TPU v7x, 32 devices: a whole 2x2x4 slice. The times are simulated.
32 devices in a mesh: dp: 2 (over x), expert: 4 (over z), mp: 4 (over y, core).
Axes of the slice: x: 2, y: 2, z: 4, core: 2. Of those that a mesh axis runs over, the one named last changes fastest.
Arguments:
- tokens: bfloat16 [128, 4096], P(('dp', 'expert', 'mp')), may hold values from -6 to 6
- probes: bfloat16 [2, 128, 4096], P(None, ('dp', 'expert', 'mp')), may hold values from -6 to 6
- cotangent: bfloat16 [128, 4096], P(('dp', 'expert', 'mp')), may hold values from -0.119628906 to 0.119628906
- expert_ids: int32 [128, 2], P(('dp', 'expert', 'mp')), may hold values from 0 to 3, all different within a row; in each aligned block of 4 rows (0 to 3, 4 to 7, ...) at most 4 rows name the same one
- combine: float32 [128, 2], P(('dp', 'expert', 'mp')), may hold values from 0.2 to 1
- w_gate: bfloat16 [4, 4096, 14336], P('expert', None, ('dp', 'mp')), may hold values from -0.09375 to 0.09375
- w_up: bfloat16 [4, 4096, 14336], P('expert', None, ('dp', 'mp')), may hold values from -0.09375 to 0.09375
- w_down: bfloat16 [4, 14336, 4096], P('expert', ('dp', 'mp')), may hold values from -0.046875 to 0.046875
Outputs:
- quad: float32 [2, 128], P(None, ('dp', 'expert', 'mp'))
Inputs may be any that keep to these rules, and one draw needn't show every extreme that they name: `expert_ids`: each token names 2 different experts. In each aligned block of 4 tokens (the tokens of one device) no expert is named by more than 4 of them, and some block reaches 4.
All inputs are finite; a program needn't handle non-finite values.
Results may differ from a plain program's by a relative error of at most 0.003.
Values may be sent and summed in bfloat16 or wider, within the bound.
No kernel may reach another device: no remote copies, remote signals or barrier semaphores. Data moves between devices by JAX's collectives and lax.ppermute only.
A program may use at most 128 MiB of HBM per device.

v0:
```python
import jax
import jax.numpy as jnp
from jax import lax
from jax.sharding import PartitionSpec as P


def silu_slopes(preact):
    squash = jax.nn.sigmoid(preact)
    first_slope = squash * (1.0 + preact * (1.0 - squash))
    second_slope = squash * (1.0 - squash) * (2.0 + preact * (1.0 - 2.0 * squash))
    return (first_slope, second_slope)


def on_device(tokens, probes, cotangent, expert_ids, combine, w_gate, w_up, w_down):
    tok_dev, model_width = tokens.shape
    probe_count = probes.shape[0]
    top_count = expert_ids.shape[1]
    experts = lax.axis_size("expert") * w_gate.shape[0]
    capacity = 2 * max(1, tok_dev * top_count // experts)
    routed = tok_dev * top_count
    flat_ids = expert_ids.reshape(routed)
    positions = jnp.arange(routed, dtype=jnp.int32)
    same_expert = flat_ids[:, None] == flat_ids[None, :]
    before = positions[None, :] < positions[:, None]
    slot_index = jnp.sum((same_expert & before).astype(jnp.int32), axis=1)
    expert_hot = flat_ids[:, None] == jnp.arange(experts, dtype=jnp.int32)[None, :]
    slot_hot = slot_index[:, None] == jnp.arange(capacity, dtype=jnp.int32)[None, :]
    placing = (expert_hot[:, :, None] & slot_hot[:, None, :]).reshape(routed, experts * capacity)
    scaled = (
        combine.reshape(routed, 1) * jnp.repeat(cotangent.astype(jnp.float32), top_count, axis=0)
    ).astype(jnp.bfloat16)
    stacked = jnp.repeat(jnp.concatenate([tokens[None], probes], axis=0), top_count, axis=1)
    stacked = jnp.concatenate([stacked, scaled[None]], axis=0)
    outgoing = jnp.einsum(
        "nk,rnd->rkd", placing.astype(jnp.bfloat16), stacked, preferred_element_type=jnp.float32
    ).astype(jnp.bfloat16)
    outgoing = outgoing.reshape(probe_count + 2, experts, capacity, model_width)
    arrived = lax.all_to_all(outgoing, "expert", split_axis=1, concat_axis=1, tiled=True)
    arrived = arrived.reshape(probe_count + 2, experts * capacity, model_width)
    gate_local = w_gate[0]
    up_local = w_up[0]
    down_local = w_down[0]
    block_rows = lax.all_gather(arrived, ("dp", "mp"), axis=1, tiled=True)
    row_count = block_rows.shape[1]
    base_rows = block_rows[0]
    tangent = block_rows[1 : probe_count + 1].reshape(probe_count * row_count, model_width)
    readout_rows = block_rows[probe_count + 1]
    gate_pre = jnp.dot(base_rows, gate_local, preferred_element_type=jnp.float32)
    up_pre = jnp.dot(base_rows, up_local, preferred_element_type=jnp.float32)
    readout = lax.dot_general(
        readout_rows, down_local, (((1,), (1,)), ((), ())), preferred_element_type=jnp.float32
    )
    gate_tan = jnp.dot(tangent, gate_local, preferred_element_type=jnp.float32).reshape(
        probe_count, row_count, -1
    )
    up_tan = jnp.dot(tangent, up_local, preferred_element_type=jnp.float32).reshape(
        probe_count, row_count, -1
    )
    first_slope, second_slope = silu_slopes(gate_pre)
    curved = second_slope * gate_tan * gate_tan * up_pre + 2.0 * first_slope * gate_tan * up_tan
    partial_quad = jnp.sum(curved * readout, axis=2)
    spread = partial_quad.reshape(probe_count, -1, experts, capacity)
    swapped = lax.all_to_all(spread, "expert", split_axis=2, concat_axis=2, tiled=True)
    returned_table = lax.psum_scatter(swapped, ("dp", "mp"), scatter_dimension=1, tiled=True)
    returned_table = returned_table.reshape(probe_count, experts * capacity)
    per_choice = jnp.dot(
        returned_table, placing.astype(jnp.float32).T, precision=lax.Precision.HIGHEST
    )
    return jnp.sum(per_choice.reshape(probe_count, tok_dev, top_count), axis=2)


def solution(mesh):
    in_specs = (
        P(("dp", "expert", "mp"), None),
        P(None, ("dp", "expert", "mp"), None),
        P(("dp", "expert", "mp"), None),
        P(("dp", "expert", "mp"), None),
        P(("dp", "expert", "mp"), None),
        P("expert", None, ("dp", "mp")),
        P("expert", None, ("dp", "mp")),
        P("expert", ("dp", "mp"), None),
    )
    out_specs = P(None, ("dp", "expert", "mp"))
    return jax.shard_map(
        on_device, mesh=mesh, in_specs=in_specs, out_specs=out_specs, check_vma=False
    )
```

profile of v0, /device:TPU:0, one launch (start us, length us, event | category | flops | bytes accessed | tf_op | source)
XLA Modules:
  0.0 151.4 jit_solution(9629628665399387584)
XLA Ops:
  6.5 0.0 all-gather.2.cloned.1.call-start
  6.5 0.8 copy.29
  7.3 0.1 eq.49
  7.4 0.2 convert_reduce_fusion
  7.6 0.1 iota_compare_fusion
  7.6 0.1 broadcast_and_fusion
  7.7 0.1 copy.30
  7.9 0.8 copy.28
  8.6 0.1 mul.76
  8.7 0.9 pad_maximum_fusion
  9.6 0.1 broadcast_in_dim.7
  9.8 0.1 reshape.132
  9.8 0.8 broadcast_in_dim.8
  10.6 0.1 reshape.133
  10.7 0.1 multiply_convert_fusion
  10.8 0.3 fusion.10
  11.1 0.2 reshape.134
  11.3 0.2 copy.32
  11.5 20.6 %all_to_all.10 = bf16[4,4,4,4096]{3,2,0,1:T(4,128)(2,1)S(1)} all-to-all(bf16[4,4,4,4096]{3,2,0,1:T(4,128)(2,1)S(1)} %copy.32), channel_id=1, replica_groups=mesh['dp'=2,'expert'=4,'mp'=4] {'expert'}, dimensions={1} | all-to-all | bytes 1048576 | tf_op jit(solution)/shard_map/all_to_all | solution.py:38
  32.2 0.2 copy.33
  32.4 0.9 reshape.135
  33.3 0.0 all-gather.2.cloned.1.call-update
  33.3 35.8 %all-gather.2.cloned.1.call-done = bf16[4,128,4096]{2,1,0:T(8,128)(2,1)} async-done(((bf16[4,16,4096]{2,1,0:T(8,128)(2,1)}), bf16[4,128,4096]{2,1,0:T(8,128)(2,1)}) %all-gather.2.cloned.1.call-update) | async-done | bytes 4194320 | tf_op jit(solution)/shard_map/all_gather | solution.py:43
  69.2 0.0 copy-start
  69.2 8.7 %fusion.6 = f32[2,128,1792]{2,1,0:T(8,128)S(1)} fusion(bf16[4,128,4096]{2,1,0:T(8,128)(2,1)} %all-gather.2.cloned.1.call-done, bf16[1,4096,1792]{2,1,0:T(8,128)(2,1)} %param.13), kind=kOutput, calls=%fused_computation.6 | convolution fusion | flops 3758096384 | bytes 20709376 | tf_op jit(solution)/shard_map/dot_general | solution.py:53
  77.9 0.0 copy-done
  77.9 0.0 slice-start.3
  77.9 9.5 %fusion.24 = (f32[128,1792]{1,0:T(8,128)S(1)}, f32[128,1792]{1,0:T(8,128)}) fusion(bf16[1,4096,1792]{2,1,0:T(8,128)(2,1)} %param.13, bf16[4,128,4096]{2,1,0:T(8,128)(2,1)S(1)} %copy-done), kind=kOutput, calls=%fused_computation.23 | convolution fusion | flops 1882259456 | bytes 17563648 | tf_op jit(solution)/shard_map/dot_general | solution.py:48
  87.4 0.0 slice-done
  87.4 0.0 slice-done.1
  87.4 0.0 slice-done.2
  87.4 0.0 slice-done.3
  87.5 2.2 %fusion.4 = f32[128,1792]{1,0:T(8,128)S(1)} fusion(bf16[1,4096,1792]{2,1,0:T(8,128)(2,1)S(1)} %bitcast.48, bf16[4,128,4096]{2,1,0:T(8,128)(2,1)S(1)} %copy-done), kind=kOutput, calls=%fused_computation.4 | convolution fusion | flops 1879048192 | bytes 16646144 | tf_op jit(solution)/shard_map/dot_general | solution.py:49
  89.6 10.1 %fusion = f32[128,1792]{1,0:T(8,128)S(1)} fusion(bf16[1,1792,4096]{2,1,0:T(8,128)(2,1)} %param.15, bf16[4,128,4096]{2,1,0:T(8,128)(2,1)S(1)} %copy-done), kind=kOutput, calls=%fused_computation | convolution fusion | flops 1879048192 | bytes 16646144 | tf_op jit(solution)/shard_map/dot_general | solution.py:50
  99.8 0.0 copy-start.1
  99.8 9.7 %fusion.21 = f32[2,128]{1,0:T(2,128)S(1)} fusion(bf16[4,128,4096]{2,1,0:T(8,128)(2,1)S(1)} %copy-done, bf16[1,4096,1792]{2,1,0:T(8,128)(2,1)} %param.14, f32[2,128,1792]{2,1,0:T(8,128)S(1)} %fusion.6, f32[128,1792]{1,0:T(8,128)S(1)} %fusion, f32[128,1792]{1,0:T(8,128)} %get-tuple-element.6, f32[128,1792]{1,0:T(8,128)S(1)} %fusion.4, ...), kind=kOutput, calls=%fused_computation.17 | convolution fusion | flops 3761766144 | bytes 24380416 | tf_op jit(solution)/shard_map/dot_general | solution.py:56
  109.5 0.1 reshape.136
  109.6 0.7 copy.34
  110.3 4.6 %all-to-all-start.1 = ((f32[2,8,4,4]{1,3,0,2:T(4,128)}), f32[2,8,4,4]{1,3,0,2:T(4,128)S(1)}, u32[]{:S(2)}, u32[]{:S(2)}) async-start(f32[2,8,4,4]{1,3,0,2:T(4,128)} %copy.34), calls=%async_computation.1 | async-start | bytes 32768 | tf_op jit(solution)/shard_map/all_to_all | solution.py:63
  114.9 0.1 and.35
  115.0 0.0 copy-done.1
  115.0 0.6 dynamic-slice
  115.6 4.9 %all-to-all-done.1 = f32[2,8,4,4]{1,3,0,2:T(4,128)S(1)} async-done(((f32[2,8,4,4]{1,3,0,2:T(4,128)}), f32[2,8,4,4]{1,3,0,2:T(4,128)S(1)}, u32[]{:S(2)}, u32[]{:S(2)}) %all-to-all-start.1) | async-done | bytes 1056 | tf_op jit(solution)/shard_map/all_to_all | solution.py:63
  120.6 0.1 copy.35
  120.7 22.3 %all-reduce = f32[2,8,4,4]{3,2,1,0:T(4,128)S(1)} all-reduce(f32[2,8,4,4]{3,2,1,0:T(4,128)S(1)} %copy.35), channel_id=2, replica_groups=mesh['dp'=2,'expert'=4,'mp'=4] {'dp','mp'}, use_global_device_ids=true, to_apply=%region_2.0.clone | all-reduce | flops 256 | bytes 2048
  143.0 0.6 constant_dynamic-slice_fusion
  143.7 0.1 reshape.141
  143.8 0.8 convolution_reduce_fusion
  (4 shorter events, 0.0 us)
Async XLA Ops:
  6.5 62.6 %all-gather.2.cloned.1.call-start = ((), (), s32[]{:S(2)}) async-start(), calls=%async_computation.2 | async-start | bytes 4718592 | tf_op jit(solution)/shard_map/all_gather | solution.py:43
  69.2 8.8 %copy-start = (bf16[4,128,4096]{2,1,0:T(8,128)(2,1)S(1)}, bf16[4,128,4096]{2,1,0:T(8,128)(2,1)}, u32[]{:S(2)}) copy-start(bf16[4,128,4096]{2,1,0:T(8,128)(2,1)} %all-gather.2.cloned.1.call-done) | copy-start | bytes 12582916
  69.2 18.3 %slice-start = ((s8[14680064]{0:T(1024)(128)(4,1)}), s8[4194304]{0:T(1024)(128)(4,1)S(1)}, s32[]{:S(2)}) async-start(s8[14680064]{0:T(1024)(128)(4,1)} %bitcast.47), calls=%async_computation.3 | async-start | bytes 8388608
  69.2 18.3 %slice-start.1 = ((s8[14680064]{0:T(1024)(128)(4,1)}), s8[4194304]{0:T(1024)(128)(4,1)S(1)}, s32[]{:S(2)}) async-start(s8[14680064]{0:T(1024)(128)(4,1)} %bitcast.47), calls=%async_computation.4 | async-start | bytes 8388608
  69.2 18.3 %slice-start.2 = ((s8[14680064]{0:T(1024)(128)(4,1)}), s8[4194304]{0:T(1024)(128)(4,1)S(1)}, s32[]{:S(2)}) async-start(s8[14680064]{0:T(1024)(128)(4,1)} %bitcast.47), calls=%async_computation.5 | async-start | bytes 8388608
  77.9 9.5 %slice-start.3 = ((s8[14680064]{0:T(1024)(128)(4,1)}), s8[2097152]{0:T(1024)(128)(4,1)S(1)}, s32[]{:S(2)}) async-start(s8[14680064]{0:T(1024)(128)(4,1)} %bitcast.47), calls=%async_computation.6 | async-start | bytes 4194304
  99.8 15.2 %copy-start.1 = (u32[32]{0:T(128)S(1)}, u32[32]{0:T(128)}, u32[]{:S(2)}) copy-start(u32[32]{0:T(128)} %constant.18) | copy-start | bytes 388
  110.3 10.2 %all-to-all-start.1 = ((f32[2,8,4,4]{1,3,0,2:T(4,128)}), f32[2,8,4,4]{1,3,0,2:T(4,128)S(1)}, u32[]{:S(2)}, u32[]{:S(2)}) async-start(f32[2,8,4,4]{1,3,0,2:T(4,128)} %copy.34), calls=%async_computation.1 | async-start | bytes 32768 | tf_op jit(solution)/shard_map/all_to_all | solution.py:63
Sparse Core Ops, SparseCore 0:
  33.4 35.6 all-gather.1
where the time goes:
time: 152 us; the launch traced here: 151 us
  blocking collectives  43 us (28%)
  matrix products  41.3 us (27%)
  waiting for transfers between devices  40.8 us (27%)
  between operations  13.5 us (9%)
  local copies, waits for them, and re-layouts  6.85 us (5%)
  starting transfers between devices  4.6 us (3%)
    all_gather x1, waiting for transfers between devices, on_device(): block_rows = lax.all_gather(arrived, ('dp', 'mp'), axis=1, tiled=True)  35.8 us
    unnamed x1, blocking collectives  22.3 us
    all_to_all x1, blocking collectives, on_device(): lax.all_to_all(outgoing, 'expert', split_axis=1, concat_axis=1, tiled=True)  20.6 us
    dot_general x1, matrix products, on_device(): lax.dot_general(readout_rows, down_local, (((1,), (1,)), ((), ())), prefe...  10.1 us
    dot_general x1, matrix products, on_device(): jnp.dot(tangent, up_local, preferred_element_type=jnp.float32)  9.69 us
    dot_general x1, matrix products, on_device(): jnp.dot(base_rows, gate_local, preferred_element_type=jnp.float32)  9.49 us
    dot_general x1, matrix products, on_device(): jnp.dot(tangent, gate_local, preferred_element_type=jnp.float32)  8.75 us
    all_to_all x1, waiting for transfers between devices, on_device(): lax.all_to_all(spread, 'expert', split_axis=2, concat_axis=2, tiled=True)  4.94 us
  transfers between devices with their start and end apart: 2, of which 2 were waited for; matrix products, arithmetic and copies ran while one was open for 0% of the time, Pallas kernels for 0%

commit v1 on v0

--- a/solution.py
+++ b/solution.py
@@ -1,7 +1,16 @@
 import jax
 import jax.numpy as jnp
+import numpy as np
 from jax import lax
+from jax.experimental import pallas as pl
+from jax.experimental.pallas import tpu as pltpu
+from jax.sharding import Mesh
 from jax.sharding import PartitionSpec as P
+
+LANES = 128
+FF_TILE = 256
+KINDS = 4
+VMEM_ROWS = 16 * 1024 * 1024
 
 
 def silu_slopes(preact):
@@ -11,7 +20,7 @@
     return (first_slope, second_slope)
 
 
-def on_device(tokens, probes, cotangent, expert_ids, combine, w_gate, w_up, w_down):
+def routed_on_device(tokens, probes, cotangent, expert_ids, combine, w_gate, w_up, w_down):
     tok_dev, model_width = tokens.shape
     probe_count = probes.shape[0]
     top_count = expert_ids.shape[1]
@@ -69,6 +78,232 @@
     return jnp.sum(per_choice.reshape(probe_count, tok_dev, top_count), axis=2)
 
 
+class Layout:
+    def __init__(self, mesh):
+        self.dp = mesh.shape["dp"]
+        self.expert = mesh.shape["expert"]
+        self.core = 2
+        self.y = mesh.shape["mp"] // self.core
+        self.count = mesh.size
+
+    def pairs(self, dx, dz, dy, dc):
+        out = []
+        for x in range(self.dp):
+            for z in range(self.expert):
+                for y in range(self.y):
+                    for c in range(self.core):
+                        src = self.index(x, z, y, c)
+                        dst = self.index(
+                            (x + dx) % self.dp,
+                            (z + dz) % self.expert,
+                            (y + dy) % self.y,
+                            (c + dc) % self.core,
+                        )
+                        out.append((src, dst))
+        return out
+
+    def index(self, x, z, y, c):
+        return ((x * self.expert + z) * self.y + y) * self.core + c
+
+
+AXES = ("dp", "expert", "mp")
+
+
+def make_fast(mesh, lay):
+    z_shifts = [0] + [k for k in range(1, lay.expert)]
+    plane_shifts = [(dx, dy) for dx in range(lay.dp) for dy in range(lay.y)]
+    offsets = [(dx, dz, dy) for (dx, dy) in plane_shifts for dz in z_shifts]
+
+    def send(block, dx, dz, dy, dc):
+        if dx == dz == dy == dc == 0:
+            return block
+        return lax.ppermute(block, AXES, lay.pairs(dx, dz, dy, dc))
+
+    def gather(block):
+        column = jnp.concatenate([send(block, 0, dz, 0, 0) for dz in z_shifts], axis=0)
+        mine = jnp.concatenate([send(column, dx, 0, dy, 0) for dx, dy in plane_shifts], axis=0)
+        return mine, send(mine, 0, 0, 0, 1)
+
+    def pack(tokens, probes, cotangent, expert_ids, combine):
+        tok_dev, width = tokens.shape
+        rows = jnp.concatenate([tokens[None], probes, cotangent[None]], axis=0)
+        rows = rows.reshape(KINDS * tok_dev, width)
+        high = lax.reduce_precision(combine, 8, 7)
+        rest = combine - high
+        mid = lax.reduce_precision(rest, 8, 7)
+        low = rest - mid
+        meta = jnp.concatenate([expert_ids.astype(jnp.float32), high, mid, low], axis=1)
+        meta = jnp.pad(meta, ((0, rows.shape[0] - tok_dev), (0, LANES - meta.shape[1])))
+        return jnp.concatenate([rows, meta.astype(jnp.bfloat16)], axis=1)
+
+    def on_device(tokens, probes, cotangent, expert_ids, combine, w_gate, w_up, w_down):
+        tok_dev, width = tokens.shape
+        top = expert_ids.shape[1]
+        block = pack(tokens, probes, cotangent, expert_ids, combine)[None]
+        mine, other = gather(block)
+        partial = contract(mine, other, w_gate[0], w_up[0], w_down[0], tok_dev, top)
+        swapped = lax.all_to_all(partial, AXES, split_axis=0, concat_axis=0, tiled=True)
+        total = jnp.sum(swapped, axis=0)
+        return total[: probes.shape[0] * tok_dev].reshape(probes.shape[0], tok_dev)
+
+    def contract(mine, other, w_gate, w_up, w_down, tok_dev, top):
+        half = mine.shape[0]
+        width = w_gate.shape[0]
+        ff = w_gate.shape[1]
+        tiles = ff // FF_TILE
+        rows = 2 * half * tok_dev
+        group = 16 // tok_dev
+        col = 512
+        probe_count = KINDS - 2
+
+        def body(mine_ref, other_ref, wg, wu, wd, out_ref, lhs, wts, meta, gbuf, ubuf, dbuf, acc, sems):
+            def copies(i, slot):
+                at = pl.multiple_of(i * FF_TILE, FF_TILE)
+                return (
+                    pltpu.make_async_copy(wg.at[:, pl.ds(at, FF_TILE)], gbuf.at[slot], sems.at[0, slot]),
+                    pltpu.make_async_copy(wu.at[:, pl.ds(at, FF_TILE)], ubuf.at[slot], sems.at[1, slot]),
+                    pltpu.make_async_copy(wd.at[pl.ds(at, FF_TILE), :], dbuf.at[slot], sems.at[2, slot]),
+                )
+
+            for slot in range(2):
+                for c in copies(slot, slot):
+                    c.start()
+
+            upper = lax.broadcasted_iota(jnp.int32, (8, LANES), 0) < tok_dev
+
+            def split(ref, g, at, size):
+                pieces = [[] for _ in range(KINDS)]
+                mask = lax.broadcasted_iota(jnp.int32, (8, size), 0) < tok_dev
+                for pair in range(group // 2):
+                    a = ref[g + 2 * pair, :, pl.ds(at, size)].astype(jnp.float32)
+                    b = ref[g + 2 * pair + 1, :, pl.ds(at, size)].astype(jnp.float32)
+                    for h in range(2):
+                        ah = a[8 * h : 8 * h + 8]
+                        bh = b[8 * h : 8 * h + 8]
+                        pieces[2 * h].append(jnp.where(mask, ah, pltpu.roll(bh, tok_dev, 0)))
+                        pieces[2 * h + 1].append(jnp.where(mask, pltpu.roll(ah, tok_dev, 0), bh))
+                return [jnp.concatenate(p, axis=0) for p in pieces]
+
+            expert = lax.axis_index("expert").astype(jnp.float32)
+            for n, ref in enumerate((mine_ref, other_ref)):
+                def take(i, _, n=n, ref=ref):
+                    base = pl.multiple_of((n * half + i * group) * tok_dev, 16)
+                    tags = split(ref, i * group, width, LANES)[0]
+                    weight = jnp.zeros((16, 1), jnp.float32)
+                    for j in range(top):
+                        value = tags[:, top + j : top + j + 1] + tags[:, 2 * top + j : 2 * top + j + 1]
+                        value = value + tags[:, 3 * top + j : 3 * top + j + 1]
+                        weight = weight + jnp.where(tags[:, j : j + 1] == expert, value, 0.0)
+                    for k in range(width // col):
+                        parts = split(ref, i * group, k * col, col)
+                        for kind in range(KINDS - 1):
+                            lhs[pl.ds(kind * rows + base, 16), pl.ds(k * col, col)] = parts[kind].astype(jnp.bfloat16)
+                        lhs[pl.ds((KINDS - 1) * rows + base, 16), pl.ds(k * col, col)] = (
+                            weight * parts[KINDS - 1]
+                        ).astype(jnp.bfloat16)
+                    return 0
+
+                lax.fori_loop(0, half // group, take, 0)
+
+            acc[...] = jnp.zeros(acc.shape, jnp.float32)
+
+            def tile(i, _):
+                slot = lax.rem(i, 2)
+                for c in copies(i, slot):
+                    c.wait()
+                split_at = (KINDS - 1) * rows
+                gate = jnp.dot(lhs[:split_at, :], gbuf[slot], preferred_element_type=jnp.float32)
+                up = jnp.dot(lhs[:split_at, :], ubuf[slot], preferred_element_type=jnp.float32)
+                read = lax.dot_general(
+                    lhs[split_at:, :], dbuf[slot], (((1,), (1,)), ((), ())), preferred_element_type=jnp.float32
+                )
+
+                @pl.when(i + 2 < tiles)
+                def _():
+                    for c in copies(i + 2, slot):
+                        c.start()
+
+                first, second = silu_slopes(gate[:rows])
+                second = second * up[:rows] * read
+                first = 2.0 * first * read
+                for p in range(probe_count):
+                    gate_tan = gate[(p + 1) * rows : (p + 2) * rows]
+                    up_tan = up[(p + 1) * rows : (p + 2) * rows]
+                    term = gate_tan * (second * gate_tan + first * up_tan)
+                    for h in range(FF_TILE // LANES):
+                        acc[p] += term[:, h * LANES : (h + 1) * LANES]
+                return 0
+
+            lax.fori_loop(0, tiles, tile, 0)
+
+            def device_of(block):
+                x = lax.axis_index("dp")
+                z = lax.axis_index("expert")
+                m = lax.axis_index("mp")
+                y = m // lay.core
+                c = m % lay.core
+                out = jnp.zeros(block.shape, jnp.int32)
+                for j, (dx, dz, dy) in enumerate(offsets):
+                    for dc in range(lay.core):
+                        src = lay.index(
+                            (x + lay.dp - dx) % lay.dp,
+                            (z + lay.expert - dz) % lay.expert,
+                            (y + lay.y - dy) % lay.y,
+                            (c + lay.core - dc) % lay.core,
+                        )
+                        out = jnp.where(block == dc * half + j, src, out)
+                return out
+
+            row_block = lax.broadcasted_iota(jnp.int32, (2 * half, rows), 1) // tok_dev
+            hot = device_of(row_block) == lax.broadcasted_iota(jnp.int32, (2 * half, rows), 0)
+            row = lax.broadcasted_iota(jnp.int32, (rows, LANES), 0) % tok_dev
+            lane = lax.broadcasted_iota(jnp.int32, (rows, LANES), 1)
+            spread = jnp.zeros((rows, LANES), jnp.float32)
+            for p in range(probe_count):
+                value = jnp.sum(acc[p], axis=1, keepdims=True)
+                spread = spread + jnp.where(lane == row + p * tok_dev, value, 0.0)
+            out_ref[...] = jnp.dot(
+                hot.astype(jnp.float32), spread, precision=lax.Precision.HIGHEST, preferred_element_type=jnp.float32
+            )
+
+        vmem = pl.BlockSpec(memory_space=pltpu.VMEM)
+        hbm = pl.BlockSpec(memory_space=pl.ANY)
+        return pl.pallas_call(
+            body,
+            out_shape=jax.ShapeDtypeStruct((2 * half, LANES), jnp.float32),
+            in_specs=[vmem, vmem, hbm, hbm, hbm],
+            out_specs=vmem,
+            scratch_shapes=[
+                pltpu.VMEM((KINDS * rows, width), jnp.bfloat16),
+                pltpu.VMEM((8, LANES), jnp.float32),
+                pltpu.VMEM((8, LANES), jnp.float32),
+                pltpu.VMEM((2, width, FF_TILE), jnp.bfloat16),
+                pltpu.VMEM((2, width, FF_TILE), jnp.bfloat16),
+                pltpu.VMEM((2, FF_TILE, width), jnp.bfloat16),
+                pltpu.VMEM((probe_count, rows, LANES), jnp.float32),
+                pltpu.SemaphoreType.DMA((3, 2)),
+            ],
+            compiler_params=pltpu.CompilerParams(vmem_limit_bytes=40 * 1024 * 1024),
+            name="contract",
+        )(mine, other, w_gate, w_up, w_down)
+
+    return on_device
+
+
+def fits(mesh, args):
+    tokens, probes, w_gate = args[0], args[1], args[5]
+    rows = (probes.shape[0] + 2) * tokens.shape[0]
+    tok_dev = tokens.shape[0] // mesh.size
+    return (
+        mesh.shape["mp"] % 2 == 0
+        and w_gate.shape[0] == mesh.shape["expert"]
+        and probes.shape[0] + 2 == KINDS
+        and tok_dev == 4
+        and 4 * rows * tokens.shape[1] <= VMEM_ROWS
+        and w_gate.shape[2] % (mesh.shape["dp"] * mesh.shape["mp"] * FF_TILE) == 0
+    )
+
+
 def solution(mesh):
     in_specs = (
         P(("dp", "expert", "mp"), None),
@@ -81,6 +316,11 @@
         P("expert", ("dp", "mp"), None),
     )
     out_specs = P(None, ("dp", "expert", "mp"))
-    return jax.shard_map(
-        on_device, mesh=mesh, in_specs=in_specs, out_specs=out_specs, check_vma=False
-    )
+
+    def program(*args):
+        body = make_fast(mesh, Layout(mesh)) if fits(mesh, args) else routed_on_device
+        return jax.shard_map(
+            body, mesh=mesh, in_specs=in_specs, out_specs=out_specs, check_vma=False
+        )(*args)
+
+    return program

time: 152 us -> 82.3 us (0.54)
  matrix products: 41.3 us -> 0 us
  blocking collectives: 43 us -> 12.7 us
  Pallas kernels: 0 us -> 20.1 us
  between operations: 13.5 us -> 0.06 us
  starting transfers between devices: 4.6 us -> 10.7 us
  waiting for transfers between devices: 40.8 us -> 35 us
  local copies, waits for them, and re-layouts: 6.85 us -> 2.4 us
    dot_general x7 -> x0, matrix products: 41.3 us -> none  [the longest x1 10.1 us: on_device(): lax.dot_general(readout_rows, down_local, (((1,), (1,)), ((), ())), prefe...]
    all_gather x1 -> x0, waiting for transfers between devices: 35.8 us -> none  [on_device(): block_rows = lax.all_gather(arrived, ('dp', 'mp'), axis=1, tiled=True)]
    ppermute x0 -> x7, waiting for transfers between devices: none -> 35 us  [send(): return lax.ppermute(block, AXES, lay.pairs(dx, dz, dy, dc))]
    unnamed x1 -> x0, blocking collectives: 22.3 us -> none
    pallas_call x0 -> x1, Pallas kernels: none -> 20.1 us  [contract(): pl.pallas_call(body, out_shape=jax.ShapeDtypeStruct((2 * half, LANES), jn...]
    ppermute x0 -> x7, starting transfers between devices: none -> 10.7 us  [send(): return lax.ppermute(block, AXES, lay.pairs(dx, dz, dy, dc))]
    all_to_all x1, blocking collectives: 20.6 us -> 12.7 us  [on_device(): lax.all_to_all(partial, AXES, split_axis=0, concat_axis=0, tiled=True)]
    all_to_all x1 -> x0, waiting for transfers between devices: 4.94 us -> none  [on_device(): lax.all_to_all(spread, 'expert', split_axis=2, concat_axis=2, tiled=True)]
  transfers between devices with their start and end apart: 2 -> 7, of which waited for: 2 -> 6; matrix products, arithmetic and copies ran while one was open for 0% -> 0% of each run, Pallas kernels for 0% -> 0%
where the time goes in v1:
time: 82.3 us; the launch traced here: 82.1 us
  waiting for transfers between devices  35 us (43%)
  Pallas kernels  20.1 us (24%)
  blocking collectives  12.7 us (15%)
  starting transfers between devices  10.7 us (13%)
  local copies, waits for them, and re-layouts  2.4 us (3%)
  other arithmetic  1.21 us (1%)
    ppermute x7, waiting for transfers between devices, send(): return lax.ppermute(block, AXES, lay.pairs(dx, dz, dy, dc))  35 us
    pallas_call x1, Pallas kernels, contract(): pl.pallas_call(body, out_shape=jax.ShapeDtypeStruct((2 * half, LANES), jn...  20.1 us
    all_to_all x1, blocking collectives, on_device(): lax.all_to_all(partial, AXES, split_axis=0, concat_axis=0, tiled=True)  12.7 us
    ppermute x7, starting transfers between devices, send(): return lax.ppermute(block, AXES, lay.pairs(dx, dz, dy, dc))  10.7 us
    unnamed x7, local copies, waits for them, and re-layouts  1.67 us
  transfers between devices with their start and end apart: 7, of which 6 were waited for; matrix products, arithmetic and copies ran while one was open for 0% of the time, Pallas kernels for 0%

profile of v1, /device:TPU:0, one launch (start us, length us, event | category | flops | bytes accessed | tf_op | source)
XLA Modules:
  0.0 82.1 jit_solution(15318042272104233503)
XLA Ops:
  0.0 0.8 copy.13
  0.8 0.8 copy.12
  1.5 1.0 %pad_maximum_fusion.1 = bf16[4,4,4096]{2,1,0:T(4,128)(2,1)S(1)} fusion(bf16[1,4,4096]{2,1,0:T(4,128)(2,1)} %bitcast.17, bf16[2,4,4096]{2,1,0:T(4,128)(2,1)} %param.9, bf16[1,4,4096]{2,1,0:T(4,128)(2,1)} %bitcast.18), kind=kLoop, calls=%fused_computation.2 | loop fusion | flops 131072 | bytes 262144 | tf_op jit(solution)/shard_map/concatenate | solution.py:129
  2.5 0.1 fusion.8
  2.6 3.1 %collective-permute-start = (bf16[1,16,4224]{2,1,0:T(8,128)(2,1)S(1)}, bf16[1,16,4224]{2,1,0:T(8,128)(2,1)S(1)}, u32[]{:S(2)}, u32[]{:S(2)}) collective-permute-start(bf16[1,16,4224]{2,1,0:T(8,128)(2,1)S(1)} %maximum_bitcast_fusion), channel_id=1, source_target_pairs={{0,4},{1,5},{2,6},{3,7},{4,8},{5,9},{6,10},{7,11},{8,12},{9,13},{1... | collective-permute-start | bytes 405512 | tf_op jit(solution)/shard_map/ppermute | solution.py:120
  5.8 2.6 %collective-permute-start.1 = (bf16[1,16,4224]{2,1,0:T(8,128)(2,1)S(1)}, bf16[1,16,4224]{2,1,0:T(8,128)(2,1)S(1)}, u32[]{:S(2)}, u32[]{:S(2)}) collective-permute-start(bf16[1,16,4224]{2,1,0:T(8,128)(2,1)S(1)} %maximum_bitcast_fusion), channel_id=1, source_target_pairs={{0,8},{1,9},{2,10},{3,11},{4,12},{5,13},{6,14},{7,15},{8,0},{9,1},... | collective-permute-start | bytes 405512 | tf_op jit(solution)/shard_map/ppermute | solution.py:120
  8.3 1.3 %collective-permute-start.2 = (bf16[1,16,4224]{2,1,0:T(8,128)(2,1)S(1)}, bf16[1,16,4224]{2,1,0:T(8,128)(2,1)S(1)}, u32[]{:S(2)}, u32[]{:S(2)}) collective-permute-start(bf16[1,16,4224]{2,1,0:T(8,128)(2,1)S(1)} %maximum_bitcast_fusion), channel_id=1, source_target_pairs={{0,12},{1,13},{2,14},{3,15},{4,0},{5,1},{6,2},{7,3},{8,4},{9,5},{1... | collective-permute-start | bytes 405512 | tf_op jit(solution)/shard_map/ppermute | solution.py:120
  9.7 2.6 %collective-permute-done = bf16[1,16,4224]{2,1,0:T(8,128)(2,1)S(1)} collective-permute-done((bf16[1,16,4224]{2,1,0:T(8,128)(2,1)S(1)}, bf16[1,16,4224]{2,1,0:T(8,128)(2,1)S(1)}, u32[]{:S(2)}, u32[]{:S(2)}) %collective-permute-start) | collective-permute-done | bytes 135200 | tf_op jit(solution)/shard_map/ppermute | solution.py:120
  12.3 4.9 %collective-permute-done.1 = bf16[1,16,4224]{2,1,0:T(8,128)(2,1)S(1)} collective-permute-done((bf16[1,16,4224]{2,1,0:T(8,128)(2,1)S(1)}, bf16[1,16,4224]{2,1,0:T(8,128)(2,1)S(1)}, u32[]{:S(2)}, u32[]{:S(2)}) %collective-permute-start.1) | collective-permute-done | bytes 135200 | tf_op jit(solution)/shard_map/ppermute | solution.py:120
  17.2 0.0 collective-permute-done.2
  17.2 0.1 pad_maximum_fusion
  17.3 1.6 %collective-permute-start.3 = (bf16[4,16,4224]{2,1,0:T(8,128)(2,1)S(1)}, bf16[4,16,4224]{2,1,0:T(8,128)(2,1)S(1)}, u32[]{:S(2)}, u32[]{:S(2)}) collective-permute-start(bf16[4,16,4224]{2,1,0:T(8,128)(2,1)S(1)} %pad_maximum_fusion), channel_id=1, source_target_pairs={{0,2},{1,3},{2,0},{3,1},{4,6},{5,7},{6,4},{7,5},{8,10},{9,11},{10,... | collective-permute-start | bytes 1622024 | tf_op jit(solution)/shard_map/ppermute | solution.py:120
  18.9 1.5 %collective-permute-start.4 = (bf16[4,16,4224]{2,1,0:T(8,128)(2,1)S(1)}, bf16[4,16,4224]{2,1,0:T(8,128)(2,1)S(1)}, u32[]{:S(2)}, u32[]{:S(2)}) collective-permute-start(bf16[4,16,4224]{2,1,0:T(8,128)(2,1)S(1)} %pad_maximum_fusion), channel_id=1, source_target_pairs={{0,16},{1,17},{2,18},{3,19},{4,20},{5,21},{6,22},{7,23},{8,24},{9,... | collective-permute-start | bytes 1622024 | tf_op jit(solution)/shard_map/ppermute | solution.py:120
  20.4 0.5 collective-permute-start.5
  20.9 10.7 %collective-permute-done.3 = bf16[4,16,4224]{2,1,0:T(8,128)(2,1)S(1)} collective-permute-done((bf16[4,16,4224]{2,1,0:T(8,128)(2,1)S(1)}, bf16[4,16,4224]{2,1,0:T(8,128)(2,1)S(1)}, u32[]{:S(2)}, u32[]{:S(2)}) %collective-permute-start.3) | collective-permute-done | bytes 540704 | tf_op jit(solution)/shard_map/ppermute | solution.py:120
  31.7 2.4 %collective-permute-done.4 = bf16[4,16,4224]{2,1,0:T(8,128)(2,1)S(1)} collective-permute-done((bf16[4,16,4224]{2,1,0:T(8,128)(2,1)S(1)}, bf16[4,16,4224]{2,1,0:T(8,128)(2,1)S(1)}, u32[]{:S(2)}, u32[]{:S(2)}) %collective-permute-start.4) | collective-permute-done | bytes 540704 | tf_op jit(solution)/shard_map/ppermute | solution.py:120
  34.1 10.2 %collective-permute-done.5 = bf16[4,16,4224]{2,1,0:T(8,128)(2,1)S(1)} collective-permute-done((bf16[4,16,4224]{2,1,0:T(8,128)(2,1)S(1)}, bf16[4,16,4224]{2,1,0:T(8,128)(2,1)S(1)}, u32[]{:S(2)}, u32[]{:S(2)}) %collective-permute-start.5) | collective-permute-done | bytes 540704 | tf_op jit(solution)/shard_map/ppermute | solution.py:120
  44.3 0.1 collective-permute-start.6
  44.4 4.2 %collective-permute-done.6.other_ref = bf16[16,16,4224]{2,1,0:T(8,128)(2,1)S(1)} collective-permute-done((bf16[16,16,4224]{2,1,0:T(8,128)(2,1)S(1)}, bf16[16,16,4224]{2,1,0:T(8,128)(2,1)S(1)}, u32[]{:S(2)}, u32[]{:S(2)}) %collective-permute-start.6) | collective-permute-done | bytes 2162720 | tf_op jit(solution)/shard_map/ppermute | solution.py:120
  48.6 20.1 %contract.1 = f32[32,128]{1,0:T(8,128)S(1)} custom-call(bf16[16,16,4224]{2,1,0:T(8,128)(2,1)S(1)} %constant_dynamic-update-slice_fusion.mine_ref, bf16[16,16,4224]{2,1,0:T(8,128)(2,1)S(1)} %collective-permute-done.6.other_ref, bf16[4096,1792]{1,0:T(8,128)(2,1)} %bitcast.14, bf16[4096,1792]{1,0:T(8,128)(2,1)} %bitcast.15, bf16[1792,4096]{1,0:T(8,128)(2,1)} %bitcast.16), custom_call_target="tpu_custom_call" | custom-call | tf_op jit(solution)/shard_map/contract/pallas_call | solution.py:271
  68.7 12.7 %all_to_all.9 = f32[32,1,128]{2,1,0:T(1,128)S(1)} all-to-all(f32[32,1,128]{2,1,0:T(1,128)S(1)} %bitcast.13), channel_id=1, replica_groups=mesh['dp'=2,'expert'=4,'mp'=4] {'dp','expert','mp'}, dimensions={0} | all-to-all | bytes 32768 | tf_op jit(solution)/shard_map/all_to_all | solution.py:145
  81.4 0.1 reduce_sum.9
  81.5 0.6 reshape.17
  (11 shorter events, 0.3 us)
Async XLA Ops:
  2.6 9.7 %collective-permute-start = (bf16[1,16,4224]{2,1,0:T(8,128)(2,1)S(1)}, bf16[1,16,4224]{2,1,0:T(8,128)(2,1)S(1)}, u32[]{:S(2)}, u32[]{:S(2)}) collective-permute-start(bf16[1,16,4224]{2,1,0:T(8,128)(2,1)S(1)} %maximum_bitcast_fusion), channel_id=1, source_target_pairs={{0,4},{1,5},{2,6},{3,7},{4,8},{5,9},{6,10},{7,11},{8,12},{9,13},{1... | collective-permute-start | bytes 405512 | tf_op jit(solution)/shard_map/ppermute | solution.py:120
  5.8 11.5 %collective-permute-start.1 = (bf16[1,16,4224]{2,1,0:T(8,128)(2,1)S(1)}, bf16[1,16,4224]{2,1,0:T(8,128)(2,1)S(1)}, u32[]{:S(2)}, u32[]{:S(2)}) collective-permute-start(bf16[1,16,4224]{2,1,0:T(8,128)(2,1)S(1)} %maximum_bitcast_fusion), channel_id=1, source_target_pairs={{0,8},{1,9},{2,10},{3,11},{4,12},{5,13},{6,14},{7,15},{8,0},{9,1},... | collective-permute-start | bytes 405512 | tf_op jit(solution)/shard_map/ppermute | solution.py:120
  8.3 8.9 %collective-permute-start.2 = (bf16[1,16,4224]{2,1,0:T(8,128)(2,1)S(1)}, bf16[1,16,4224]{2,1,0:T(8,128)(2,1)S(1)}, u32[]{:S(2)}, u32[]{:S(2)}) collective-permute-start(bf16[1,16,4224]{2,1,0:T(8,128)(2,1)S(1)} %maximum_bitcast_fusion), channel_id=1, source_target_pairs={{0,12},{1,13},{2,14},{3,15},{4,0},{5,1},{6,2},{7,3},{8,4},{9,5},{1... | collective-permute-start | bytes 405512 | tf_op jit(solution)/shard_map/ppermute | solution.py:120
  17.3 14.3 %collective-permute-start.3 = (bf16[4,16,4224]{2,1,0:T(8,128)(2,1)S(1)}, bf16[4,16,4224]{2,1,0:T(8,128)(2,1)S(1)}, u32[]{:S(2)}, u32[]{:S(2)}) collective-permute-start(bf16[4,16,4224]{2,1,0:T(8,128)(2,1)S(1)} %pad_maximum_fusion), channel_id=1, source_target_pairs={{0,2},{1,3},{2,0},{3,1},{4,6},{5,7},{6,4},{7,5},{8,10},{9,11},{10,... | collective-permute-start | bytes 1622024 | tf_op jit(solution)/shard_map/ppermute | solution.py:120
  18.9 15.1 %collective-permute-start.4 = (bf16[4,16,4224]{2,1,0:T(8,128)(2,1)S(1)}, bf16[4,16,4224]{2,1,0:T(8,128)(2,1)S(1)}, u32[]{:S(2)}, u32[]{:S(2)}) collective-permute-start(bf16[4,16,4224]{2,1,0:T(8,128)(2,1)S(1)} %pad_maximum_fusion), channel_id=1, source_target_pairs={{0,16},{1,17},{2,18},{3,19},{4,20},{5,21},{6,22},{7,23},{8,24},{9,... | collective-permute-start | bytes 1622024 | tf_op jit(solution)/shard_map/ppermute | solution.py:120
  20.4 23.9 %collective-permute-start.5 = (bf16[4,16,4224]{2,1,0:T(8,128)(2,1)S(1)}, bf16[4,16,4224]{2,1,0:T(8,128)(2,1)S(1)}, u32[]{:S(2)}, u32[]{:S(2)}) collective-permute-start(bf16[4,16,4224]{2,1,0:T(8,128)(2,1)S(1)} %pad_maximum_fusion), channel_id=1, source_target_pairs={{0,18},{1,19},{2,16},{3,17},{4,22},{5,23},{6,20},{7,21},{8,26},{9,... | collective-permute-start | bytes 1622024 | tf_op jit(solution)/shard_map/ppermute | solution.py:120
  44.3 4.3 %collective-permute-start.6 = (bf16[16,16,4224]{2,1,0:T(8,128)(2,1)S(1)}, bf16[16,16,4224]{2,1,0:T(8,128)(2,1)S(1)}, u32[]{:S(2)}, u32[]{:S(2)}) collective-permute-start(bf16[16,16,4224]{2,1,0:T(8,128)(2,1)S(1)} %constant_dynamic-update-slice_fusion.mine_ref), channel_id=1, source_target_pairs={{0,1},{1,0},{2,3},{3,2},{4,5},{5,4},{6,7},{7,6},{8,9},{9,8},{10,11... | collective-permute-start | bytes 6488072 | tf_op jit(solution)/shard_map/ppermute | solution.py:120

commit v2 on v1

v2 whole, which is shorter than its diff:
```python
import jax
import jax.numpy as jnp
from jax import lax
from jax.experimental import pallas as pl
from jax.experimental.pallas import tpu as pltpu
from jax.sharding import PartitionSpec as P


LANES = 128
FF_TILE = 256
COLUMNS = 256
CUT = 22
SLOTS = 3
KINDS = 4
VMEM_ROWS = 16 * 1024 * 1024


def silu_slopes(preact):
    squash = jax.nn.sigmoid(preact)
    first_slope = squash * (1.0 + preact * (1.0 - squash))
    second_slope = squash * (1.0 - squash) * (2.0 + preact * (1.0 - 2.0 * squash))
    return (first_slope, second_slope)


def routed_on_device(tokens, probes, cotangent, expert_ids, combine, w_gate, w_up, w_down):
    tok_dev, model_width = tokens.shape
    probe_count = probes.shape[0]
    top_count = expert_ids.shape[1]
    experts = lax.axis_size("expert") * w_gate.shape[0]
    capacity = 2 * max(1, tok_dev * top_count // experts)
    routed = tok_dev * top_count
    flat_ids = expert_ids.reshape(routed)
    positions = jnp.arange(routed, dtype=jnp.int32)
    same_expert = flat_ids[:, None] == flat_ids[None, :]
    before = positions[None, :] < positions[:, None]
    slot_index = jnp.sum((same_expert & before).astype(jnp.int32), axis=1)
    expert_hot = flat_ids[:, None] == jnp.arange(experts, dtype=jnp.int32)[None, :]
    slot_hot = slot_index[:, None] == jnp.arange(capacity, dtype=jnp.int32)[None, :]
    placing = (expert_hot[:, :, None] & slot_hot[:, None, :]).reshape(routed, experts * capacity)
    scaled = (
        combine.reshape(routed, 1) * jnp.repeat(cotangent.astype(jnp.float32), top_count, axis=0)
    ).astype(jnp.bfloat16)
    stacked = jnp.repeat(jnp.concatenate([tokens[None], probes], axis=0), top_count, axis=1)
    stacked = jnp.concatenate([stacked, scaled[None]], axis=0)
    outgoing = jnp.einsum(
        "nk,rnd->rkd", placing.astype(jnp.bfloat16), stacked, preferred_element_type=jnp.float32
    ).astype(jnp.bfloat16)
    outgoing = outgoing.reshape(probe_count + 2, experts, capacity, model_width)
    arrived = lax.all_to_all(outgoing, "expert", split_axis=1, concat_axis=1, tiled=True)
    arrived = arrived.reshape(probe_count + 2, experts * capacity, model_width)
    gate_local = w_gate[0]
    up_local = w_up[0]
    down_local = w_down[0]
    block_rows = lax.all_gather(arrived, ("dp", "mp"), axis=1, tiled=True)
    row_count = block_rows.shape[1]
    base_rows = block_rows[0]
    tangent = block_rows[1 : probe_count + 1].reshape(probe_count * row_count, model_width)
    readout_rows = block_rows[probe_count + 1]
    gate_pre = jnp.dot(base_rows, gate_local, preferred_element_type=jnp.float32)
    up_pre = jnp.dot(base_rows, up_local, preferred_element_type=jnp.float32)
    readout = lax.dot_general(
        readout_rows, down_local, (((1,), (1,)), ((), ())), preferred_element_type=jnp.float32
    )
    gate_tan = jnp.dot(tangent, gate_local, preferred_element_type=jnp.float32).reshape(
        probe_count, row_count, -1
    )
    up_tan = jnp.dot(tangent, up_local, preferred_element_type=jnp.float32).reshape(
        probe_count, row_count, -1
    )
    first_slope, second_slope = silu_slopes(gate_pre)
    curved = second_slope * gate_tan * gate_tan * up_pre + 2.0 * first_slope * gate_tan * up_tan
    partial_quad = jnp.sum(curved * readout, axis=2)
    spread = partial_quad.reshape(probe_count, -1, experts, capacity)
    swapped = lax.all_to_all(spread, "expert", split_axis=2, concat_axis=2, tiled=True)
    returned_table = lax.psum_scatter(swapped, ("dp", "mp"), scatter_dimension=1, tiled=True)
    returned_table = returned_table.reshape(probe_count, experts * capacity)
    per_choice = jnp.dot(
        returned_table, placing.astype(jnp.float32).T, precision=lax.Precision.HIGHEST
    )
    return jnp.sum(per_choice.reshape(probe_count, tok_dev, top_count), axis=2)


class Layout:
    def __init__(self, mesh):
        self.dp = mesh.shape["dp"]
        self.expert = mesh.shape["expert"]
        self.core = 2
        self.y = mesh.shape["mp"] // self.core

    def pairs(self, dx, dz, dy, dc):
        out = []
        for x in range(self.dp):
            for z in range(self.expert):
                for y in range(self.y):
                    for c in range(self.core):
                        src = self.index(x, z, y, c)
                        dst = self.index(
                            (x + dx) % self.dp,
                            (z + dz) % self.expert,
                            (y + dy) % self.y,
                            (c + dc) % self.core,
                        )
                        out.append((src, dst))
        return out

    def index(self, x, z, y, c):
        return ((x * self.expert + z) * self.y + y) * self.core + c


AXES = ("dp", "expert", "mp")


def make_fast(lay):
    z_shifts = list(range(lay.expert))
    plane_shifts = [(dx, dy) for dx in range(lay.dp) for dy in range(lay.y)]

    def send(block, dx, dz, dy, dc):
        if dx == dz == dy == dc == 0:
            return block
        return lax.ppermute(block, AXES, lay.pairs(dx, dz, dy, dc))

    def over_z(block):
        return [send(block, 0, dz, 0, 0) for dz in z_shifts]

    def over_plane(block):
        return [send(block, dx, 0, dy, 0) for dx, dy in plane_shifts]

    def over_core(pieces):
        return [[send(piece, 0, 0, 0, dc) for piece in pieces] for dc in range(lay.core)]

    def join(pieces):
        return jnp.concatenate(pieces, axis=0)

    def pack(tokens, probes, cotangent, expert_ids, combine, cut):
        tok_dev, width = tokens.shape
        top = expert_ids.shape[1]

        def body(tok_ref, probe_ref, cot_ref, ids_ref, weight_ref, a_ref, b_ref):
            f32 = jnp.float32
            kinds = [tok_ref[...], *(probe_ref[p] for p in range(KINDS - 2)), cot_ref[...]]
            rows = jnp.concatenate([k.astype(f32) for k in kinds], axis=0).astype(jnp.bfloat16)
            a_ref[0, :, LANES:] = rows[:, :cut]
            b_ref[0] = rows[:, cut:]
            lane = lax.broadcasted_iota(jnp.int32, (tok_dev, LANES), 1)
            meta = jnp.zeros((tok_dev, LANES), f32)
            own = lax.broadcasted_iota(jnp.int32, (tok_dev, tok_dev), 0) == lax.broadcasted_iota(
                jnp.int32, (tok_dev, tok_dev), 1
            )

            def column(ref, k):
                return jnp.sum(jnp.where(own, ref[k : k + 1, :].astype(f32), 0.0), axis=1, keepdims=True)

            for k in range(top):
                rest = column(weight_ref, k)
                meta = jnp.where(lane == k, column(ids_ref, k), meta)
                for part in range(3):
                    value = rest.astype(jnp.bfloat16).astype(f32)
                    meta = jnp.where(lane == (part + 1) * top + k, value, meta)
                    rest = rest - value
            blank = jnp.zeros(((KINDS - 1) * tok_dev, LANES), f32)
            a_ref[0, :, :LANES] = jnp.concatenate([meta, blank], axis=0).astype(jnp.bfloat16)

        return pl.pallas_call(
            body,
            out_shape=(
                jax.ShapeDtypeStruct((1, KINDS * tok_dev, LANES + cut), jnp.bfloat16),
                jax.ShapeDtypeStruct((1, KINDS * tok_dev, width - cut), jnp.bfloat16),
            ),
            name="pack",
        )(tokens, probes, cotangent, expert_ids.T, combine.T)

    def on_device(tokens, probes, cotangent, expert_ids, combine, w_gate, w_up, w_down):
        return staged(tokens, probes, cotangent, expert_ids, combine, w_gate, w_up, w_down)

    def staged(tokens, probes, cotangent, expert_ids, combine, w_gate, w_up, w_down):
        tok_dev, width = tokens.shape
        probe_count = probes.shape[0]
        a, b = pack(tokens, probes, cotangent, expert_ids, combine, width * CUT // 32)
        a = join(over_z(a))
        b = join(over_plane(b))
        a = over_core(over_plane(a))
        b = over_core(over_z(b))
        partial = contract(a, b, w_gate[0], w_up[0], w_down[0], tok_dev, expert_ids.shape[1])
        swapped = lax.all_to_all(partial, AXES, split_axis=0, concat_axis=0, tiled=True)
        total = jnp.sum(swapped, axis=0)
        return total[: probe_count * tok_dev].reshape(probe_count, tok_dev)

    def contract(a, b, w_gate, w_up, w_down, tok_dev, top):
        width, ff = w_gate.shape
        tiles = ff // FF_TILE
        half = len(plane_shifts) * len(z_shifts)
        rows = 2 * half * tok_dev
        group = len(z_shifts)
        probe_count = KINDS - 2
        top_rows = (KINDS - 1) * rows
        size = group * tok_dev
        flat = [piece for core in a for piece in core] + [piece for core in b for piece in core]

        def body(*refs):
            refs = list(refs)
            pieces = [refs.pop(0) for _ in flat]
            wg, wu, wd, out_ref = [refs.pop(0) for _ in range(4)]
            lhs, gbuf, ubuf, dbuf, gate_ref, up_ref, read_ref, acc, sems = refs

            def copies(i, slot):
                at = pl.multiple_of(i * FF_TILE, FF_TILE)
                return (
                    pltpu.make_async_copy(wg.at[:, pl.ds(at, FF_TILE)], gbuf.at[slot], sems.at[0, slot]),
                    pltpu.make_async_copy(wu.at[:, pl.ds(at, FF_TILE)], ubuf.at[slot], sems.at[1, slot]),
                    pltpu.make_async_copy(wd.at[pl.ds(at, FF_TILE), :], dbuf.at[slot], sems.at[2, slot]),
                )

            for i in range(SLOTS):
                for c in copies(i, i):
                    c.start()

            def split(blocks, at, size):
                parts = [[] for _ in range(KINDS)]
                mask = lax.broadcasted_iota(jnp.int32, (8, size), 0) < tok_dev
                for (ra, ia), (rb, ib) in zip(blocks[::2], blocks[1::2]):
                    x = ra[ia, :, pl.ds(at, size)].astype(jnp.float32)
                    y = rb[ib, :, pl.ds(at, size)].astype(jnp.float32)
                    for h in range(2):
                        xh = x[8 * h : 8 * h + 8]
                        yh = y[8 * h : 8 * h + 8]
                        parts[2 * h].append(jnp.where(mask, xh, pltpu.roll(yh, tok_dev, 0)))
                        parts[2 * h + 1].append(jnp.where(mask, pltpu.roll(xh, tok_dev, 0), yh))
                return [jnp.concatenate(p, axis=0) for p in parts]

            expert = lax.axis_index("expert").astype(jnp.float32)
            count = len(plane_shifts)
            for core in range(lay.core):
                mine = pieces[core * count : (core + 1) * count]
                late = pieces[2 * count + core * group : 2 * count + (core + 1) * group]
                for j in range(count):
                    early = [(mine[j], dz) for dz in range(group)]
                    base = (core * count + j) * size
                    tags = split(early, 0, LANES)[0]
                    weight = jnp.zeros((size, 1), jnp.float32)
                    for k in range(top):
                        value = tags[:, top + k : top + k + 1] + tags[:, 2 * top + k : 2 * top + k + 1]
                        value = value + tags[:, 3 * top + k : 3 * top + k + 1]
                        weight = weight + jnp.where(tags[:, k : k + 1] == expert, value, 0.0)
                    wide = jnp.broadcast_to(weight, (size, COLUMNS))

                    def take(blocks, at, to):
                        parts = split(blocks, at, COLUMNS)
                        parts[-1] = wide * parts[-1]
                        for kind in range(KINDS):
                            lhs[pl.ds(kind * rows + base, size), pl.ds(to, COLUMNS)] = parts[kind].astype(jnp.bfloat16)

                    cut = mine[0].shape[2] - LANES
                    for k in range(cut // COLUMNS):
                        take(early, LANES + k * COLUMNS, k * COLUMNS)
                    for k in range((width - cut) // COLUMNS):
                        take([(late[dz], j) for dz in range(group)], k * COLUMNS, cut + k * COLUMNS)

            acc[...] = jnp.zeros(acc.shape, jnp.float32)

            def products(gate_w, up_w, down_w, slot):
                gate_ref[slot] = jnp.dot(lhs[:top_rows, :], gate_w, preferred_element_type=jnp.float32)
                up_ref[slot] = jnp.dot(lhs[:top_rows, :], up_w, preferred_element_type=jnp.float32)
                read_ref[slot] = lax.dot_general(
                    lhs[top_rows:, :], down_w, (((1,), (1,)), ((), ())), preferred_element_type=jnp.float32
                )

            def curve(slot):
                read = read_ref[slot]
                first, second = silu_slopes(gate_ref[slot, :rows])
                second = second * up_ref[slot, :rows] * read
                first = 2.0 * first * read
                for p in range(probe_count):
                    gate_tan = gate_ref[slot, pl.ds((p + 1) * rows, rows)]
                    up_tan = up_ref[slot, pl.ds((p + 1) * rows, rows)]
                    term = gate_tan * (second * gate_tan + first * up_tan)
                    for h in range(FF_TILE // LANES):
                        acc[p] += term[:, h * LANES : (h + 1) * LANES]

            def load(i):
                slot = lax.rem(i, SLOTS)
                for c in copies(i, slot):
                    c.wait()
                products(gbuf[slot], ubuf[slot], dbuf[slot], lax.rem(i, 2))

            def refill(i):
                @pl.when(i + SLOTS < tiles)
                def _():
                    for c in copies(i + SLOTS, lax.rem(i, SLOTS)):
                        c.start()

            load(0)
            refill(0)

            def tile(i, _):
                load(i)
                curve(lax.rem(i + 1, 2))
                refill(i)
                return 0

            lax.fori_loop(1, tiles, tile, 0)
            curve((tiles - 1) % 2)

            def device_of(block):
                x = lax.axis_index("dp")
                z = lax.axis_index("expert")
                m = lax.axis_index("mp")
                y = m // lay.core
                c = m % lay.core
                out = jnp.zeros(block.shape, jnp.int32)
                for dc in range(lay.core):
                    for j, (dx, dy) in enumerate(plane_shifts):
                        for dz in z_shifts:
                            src = lay.index(
                                (x + lay.dp - dx) % lay.dp,
                                (z + lay.expert - dz) % lay.expert,
                                (y + lay.y - dy) % lay.y,
                                (c + lay.core - dc) % lay.core,
                            )
                            out = jnp.where(block == dc * half + j * group + dz, src, out)
                return out

            block = lax.broadcasted_iota(jnp.int32, (8, rows), 1) // tok_dev
            source = device_of(block)[0:1]
            hot = source == lax.broadcasted_iota(jnp.int32, (2 * half, rows), 0)
            row = lax.broadcasted_iota(jnp.int32, (rows, LANES), 0) % tok_dev
            lane = lax.broadcasted_iota(jnp.int32, (rows, LANES), 1)
            spread = jnp.zeros((rows, LANES), jnp.float32)
            for p in range(probe_count):
                value = jnp.sum(acc[p], axis=1, keepdims=True)
                spread = spread + jnp.where(lane == row + p * tok_dev, value, 0.0)
            out_ref[...] = jnp.dot(
                hot.astype(jnp.float32), spread, precision=lax.Precision.HIGHEST, preferred_element_type=jnp.float32
            )

        vmem = pl.BlockSpec(memory_space=pltpu.VMEM)
        hbm = pl.BlockSpec(memory_space=pl.ANY)
        f32 = jnp.float32
        return pl.pallas_call(
            body,
            out_shape=jax.ShapeDtypeStruct((2 * half, LANES), f32),
            in_specs=[vmem] * len(flat) + [hbm] * 3,
            out_specs=vmem,
            scratch_shapes=[
                pltpu.VMEM((KINDS * rows, width), jnp.bfloat16),
                pltpu.VMEM((SLOTS, width, FF_TILE), jnp.bfloat16),
                pltpu.VMEM((SLOTS, width, FF_TILE), jnp.bfloat16),
                pltpu.VMEM((SLOTS, FF_TILE, width), jnp.bfloat16),
                pltpu.VMEM((2, top_rows, FF_TILE), f32),
                pltpu.VMEM((2, top_rows, FF_TILE), f32),
                pltpu.VMEM((2, rows, FF_TILE), f32),
                pltpu.VMEM((probe_count, rows, LANES), f32),
                pltpu.SemaphoreType.DMA((3, SLOTS)),
            ],
            compiler_params=pltpu.CompilerParams(vmem_limit_bytes=40 * 1024 * 1024),
            cost_estimate=pl.CostEstimate(
                flops=2 * (2 * top_rows + rows) * width * ff, bytes_accessed=3 * 2 * width * ff, transcendentals=0
            ),
            name="contract",
        )(*flat, w_gate, w_up, w_down)

    return on_device


def fits(mesh, args):
    tokens, probes, w_gate = args[0], args[1], args[5]
    rows = (probes.shape[0] + 2) * tokens.shape[0]
    tok_dev = tokens.shape[0] // mesh.size
    return (
        mesh.shape["mp"] % 2 == 0
        and w_gate.shape[0] == mesh.shape["expert"]
        and probes.shape[0] + 2 == KINDS
        and tok_dev == 4
        and 4 * rows * tokens.shape[1] <= VMEM_ROWS
        and w_gate.shape[2] % (mesh.shape["dp"] * mesh.shape["mp"] * FF_TILE) == 0
    )


def solution(mesh):
    in_specs = (
        P(("dp", "expert", "mp"), None),
        P(None, ("dp", "expert", "mp"), None),
        P(("dp", "expert", "mp"), None),
        P(("dp", "expert", "mp"), None),
        P(("dp", "expert", "mp"), None),
        P("expert", None, ("dp", "mp")),
        P("expert", None, ("dp", "mp")),
        P("expert", ("dp", "mp"), None),
    )
    out_specs = P(None, ("dp", "expert", "mp"))

    lay = Layout(mesh)

    def program(*args):
        if not fits(mesh, args):
            return jax.shard_map(
                routed_on_device, mesh=mesh, in_specs=in_specs, out_specs=out_specs, check_vma=False
            )(*args)
        step = jax.shard_map(make_fast(lay), mesh=mesh, in_specs=in_specs, out_specs=out_specs, check_vma=False)
        return step(*args)

    return program
```

time: 82.3 us -> 75.4 us (0.916)
  waiting for transfers between devices: 35 us -> 16.4 us
  starting transfers between devices: 10.7 us -> 22.7 us
  Pallas kernels: 20.1 us -> 22.1 us
  blocking collectives: 12.7 us -> 11.4 us
  other arithmetic: 1.21 us -> 0.05 us
    ppermute x7 -> x20, waiting for transfers between devices: 35 us -> 16.4 us  [send(): return lax.ppermute(block, AXES, lay.pairs(dx, dz, dy, dc))]
    ppermute x7 -> x20, starting transfers between devices: 10.7 us -> 22.7 us  [send(): return lax.ppermute(block, AXES, lay.pairs(dx, dz, dy, dc))]
    pallas_call x1 -> x2, Pallas kernels: 20.1 us -> 22.1 us  [the longest x1 20.6 us: contract(): pl.pallas_call(body, out_shape=jax.ShapeDtypeStruct((2 * half, LANES), f3...]
    all_to_all x1, blocking collectives: 12.7 us -> 11.4 us  [staged(): lax.all_to_all(partial, AXES, split_axis=0, concat_axis=0, tiled=True)]
    concatenate x3 -> x0, other arithmetic: 1.12 us -> none  [the longest x1 0.96 us: pack(): rows = jnp.concatenate([tokens[None], probes, cotangent[None]], axis=0)]
    unnamed x7 -> x6, local copies, waits for them, and re-layouts: 1.67 us -> 1.78 us
  transfers between devices with their start and end apart: 7 -> 20, of which waited for: 6 -> 6; matrix products, arithmetic and copies ran while one was open for 0% -> 2% of each run, Pallas kernels for 0% -> 0%
where the time goes in v2:
time: 75.4 us; the launch traced here: 75.2 us
  starting transfers between devices  22.7 us (30%)
  Pallas kernels  22.1 us (29%)
  waiting for transfers between devices  16.4 us (22%)
  blocking collectives  11.4 us (15%)
  local copies, waits for them, and re-layouts  2.45 us (3%)
    ppermute x20, starting transfers between devices, send(): return lax.ppermute(block, AXES, lay.pairs(dx, dz, dy, dc))  22.7 us
    pallas_call x1, Pallas kernels, contract(): pl.pallas_call(body, out_shape=jax.ShapeDtypeStruct((2 * half, LANES), f3...  20.6 us
    ppermute x20, waiting for transfers between devices, send(): return lax.ppermute(block, AXES, lay.pairs(dx, dz, dy, dc))  16.4 us
    all_to_all x1, blocking collectives, staged(): lax.all_to_all(partial, AXES, split_axis=0, concat_axis=0, tiled=True)  11.4 us
    unnamed x6, local copies, waits for them, and re-layouts  1.78 us
    pallas_call x1, Pallas kernels, pack(): pl.pallas_call(body, out_shape=(jax.ShapeDtypeStruct((1, KINDS * tok_dev,...  1.58 us
  transfers between devices with their start and end apart: 20, of which 6 were waited for; matrix products, arithmetic and copies ran while one was open for 2% of the time, Pallas kernels for 0%

profile of v2, /device:TPU:0, one launch (start us, length us, event | category | flops | bytes accessed | tf_op | source)
XLA Modules:
  0.0 75.2 jit_solution(9659691319092768545)
XLA Ops:
  0.0 1.6 %pack.1 = (bf16[1,16,2944]{2,1,0:T(8,128)(2,1)}, bf16[1,16,1280]{2,1,0:T(8,128)(2,1)}) custom-call(bf16[4,4096]{1,0:T(4,128)(2,1)} %tok_ref.1, bf16[2,4,4096]{2,1,0:T(4,128)(2,1)} %probe_ref.1, bf16[4,4096]{1,0:T(4,128)(2,1)} %cot_ref.1, s32[2,4]{1,0:T(2,128)} %bitcast.10, f32[2,4]{1,0:T(2,128)} %bitcast.11), custom_call_target="tpu_custom_call" | custom-call | tf_op jit(solution)/shard_map/pack/pallas_call | solution.py:163
  1.6 3.9 %collective-permute-start.12 = (bf16[1,16,1280]{2,1,0:T(8,128)(2,1)}, bf16[1,16,1280]{2,1,0:T(8,128)(2,1)S(1)}, u32[]{:S(2)}, u32[]{:S(2)}) collective-permute-start(bf16[1,16,1280]{2,1,0:T(8,128)(2,1)} %get-tuple-element.8), channel_id=1, source_target_pairs={{0,18},{1,19},{2,16},{3,17},{4,22},{5,23},{6,20},{7,21},{8,26},{9,... | collective-permute-start | bytes 122888 | tf_op jit(solution)/shard_map/ppermute | solution.py:120
  5.5 0.5 collective-permute-start.11
  6.0 0.0 collective-permute-start.10
  6.1 4.1 %collective-permute-start.2 = (bf16[1,16,2944]{2,1,0:T(8,128)(2,1)}, bf16[1,16,2944]{2,1,0:T(8,128)(2,1)S(1)}, u32[]{:S(2)}, u32[]{:S(2)}) collective-permute-start(bf16[1,16,2944]{2,1,0:T(8,128)(2,1)} %get-tuple-element.7), channel_id=1, source_target_pairs={{0,12},{1,13},{2,14},{3,15},{4,0},{5,1},{6,2},{7,3},{8,4},{9,5},{1... | collective-permute-start | bytes 282632 | tf_op jit(solution)/shard_map/ppermute | solution.py:120
  10.2 0.0 collective-permute-start.1
  10.2 1.0 %constant_dynamic-update-slice_fusion.3 = bf16[4,16,2944]{2,1,0:T(8,128)(2,1)S(1)} fusion(bf16[1,16,2944]{2,1,0:T(8,128)(2,1)} %get-tuple-element.7), kind=kLoop, calls=%fused_computation.3 | loop fusion | bytes 188416
  11.1 0.8 %constant_dynamic-update-slice_fusion.7 = bf16[4,16,1280]{2,1,0:T(8,128)(2,1)S(1)} fusion(bf16[1,16,1280]{2,1,0:T(8,128)(2,1)} %get-tuple-element.8), kind=kLoop, calls=%fused_computation.7 | loop fusion | bytes 81920
  11.9 0.0 collective-permute-done.10
  11.9 1.0 %collective-permute-start = (bf16[1,16,2944]{2,1,0:T(8,128)(2,1)}, bf16[1,16,2944]{2,1,0:T(8,128)(2,1)S(1)}, u32[]{:S(2)}, u32[]{:S(2)}) collective-permute-start(bf16[1,16,2944]{2,1,0:T(8,128)(2,1)} %get-tuple-element.7), channel_id=1, source_target_pairs={{0,4},{1,5},{2,6},{3,7},{4,8},{5,9},{6,10},{7,11},{8,12},{9,13},{1... | collective-permute-start | bytes 282632 | tf_op jit(solution)/shard_map/ppermute | solution.py:120
  12.9 0.0 collective-permute-done.11
  12.9 0.0 collective-permute-done.12
  12.9 0.1 collective-permute-start.16
  13.0 5.5 %collective-permute-done = bf16[1,16,2944]{2,1,0:T(8,128)(2,1)S(1)} collective-permute-done((bf16[1,16,2944]{2,1,0:T(8,128)(2,1)}, bf16[1,16,2944]{2,1,0:T(8,128)(2,1)S(1)}, u32[]{:S(2)}, u32[]{:S(2)}) %collective-permute-start) | collective-permute-done | bytes 94240 | tf_op jit(solution)/shard_map/ppermute | solution.py:120
  18.5 0.0 collective-permute-done.1
  18.5 0.0 collective-permute-done.2
  18.6 2.5 %collective-permute-start.5 = (bf16[4,16,2944]{2,1,0:T(8,128)(2,1)S(1)}, bf16[4,16,2944]{2,1,0:T(8,128)(2,1)S(1)}, u32[]{:S(2)}, u32[]{:S(2)}) collective-permute-start(bf16[4,16,2944]{2,1,0:T(8,128)(2,1)S(1)} %constant_dynamic-update-slice_fusion.refs_0_), channel_id=1, source_target_pairs={{0,18},{1,19},{2,16},{3,17},{4,22},{5,23},{6,20},{7,21},{8,26},{9,... | collective-permute-start | bytes 1130504 | tf_op jit(solution)/shard_map/ppermute | solution.py:120
  21.1 0.5 collective-permute-start.4
  21.6 0.5 collective-permute-start.3
  22.1 1.5 %collective-permute-start.15 = (bf16[4,16,1280]{2,1,0:T(8,128)(2,1)S(1)}, bf16[4,16,1280]{2,1,0:T(8,128)(2,1)S(1)}, u32[]{:S(2)}, u32[]{:S(2)}) collective-permute-start(bf16[4,16,1280]{2,1,0:T(8,128)(2,1)S(1)} %constant_dynamic-update-slice_fusion.4.refs_8_), channel_id=1, source_target_pairs={{0,12},{1,13},{2,14},{3,15},{4,0},{5,1},{6,2},{7,3},{8,4},{9,5},{1... | collective-permute-start | bytes 491528 | tf_op jit(solution)/shard_map/ppermute | solution.py:120
  23.6 0.0 collective-permute-done.16.refs_12_
  23.6 0.3 collective-permute-start.14
  23.9 4.3 %collective-permute-done.15.refs_11_ = bf16[4,16,1280]{2,1,0:T(8,128)(2,1)S(1)} collective-permute-done((bf16[4,16,1280]{2,1,0:T(8,128)(2,1)S(1)}, bf16[4,16,1280]{2,1,0:T(8,128)(2,1)S(1)}, u32[]{:S(2)}, u32[]{:S(2)}) %collective-permute-start.15) | collective-permute-done | bytes 163872 | tf_op jit(solution)/shard_map/ppermute | solution.py:120
  28.2 6.2 %collective-permute-start.13 = (bf16[4,16,1280]{2,1,0:T(8,128)(2,1)S(1)}, bf16[4,16,1280]{2,1,0:T(8,128)(2,1)S(1)}, u32[]{:S(2)}, u32[]{:S(2)}) collective-permute-start(bf16[4,16,1280]{2,1,0:T(8,128)(2,1)S(1)} %constant_dynamic-update-slice_fusion.4.refs_8_), channel_id=1, source_target_pairs={{0,4},{1,5},{2,6},{3,7},{4,8},{5,9},{6,10},{7,11},{8,12},{9,13},{1... | collective-permute-start | bytes 491528 | tf_op jit(solution)/shard_map/ppermute | solution.py:120
  34.4 2.9 %collective-permute-done.14.refs_10_ = bf16[4,16,1280]{2,1,0:T(8,128)(2,1)S(1)} collective-permute-done((bf16[4,16,1280]{2,1,0:T(8,128)(2,1)S(1)}, bf16[4,16,1280]{2,1,0:T(8,128)(2,1)S(1)}, u32[]{:S(2)}, u32[]{:S(2)}) %collective-permute-start.14) | collective-permute-done | bytes 163872 | tf_op jit(solution)/shard_map/ppermute | solution.py:120
  37.3 0.0 collective-permute-start.19
  37.3 0.0 collective-permute-done.13.refs_9_
  37.3 0.5 collective-permute-start.6
  37.9 0.0 collective-permute-done.5.refs_3_
  37.9 0.1 collective-permute-start.9
  37.9 0.0 collective-permute-done.4.refs_2_
  37.9 0.4 collective-permute-start.8
  38.4 0.0 collective-permute-done.3.refs_1_
  38.4 0.1 collective-permute-start.7
  38.4 0.3 collective-permute-done.19.refs_15_
  38.7 0.2 collective-permute-start.18
  38.9 2.2 %collective-permute-done.18.refs_14_ = bf16[4,16,1280]{2,1,0:T(8,128)(2,1)S(1)} collective-permute-done((bf16[4,16,1280]{2,1,0:T(8,128)(2,1)S(1)}, bf16[4,16,1280]{2,1,0:T(8,128)(2,1)S(1)}, u32[]{:S(2)}, u32[]{:S(2)}) %collective-permute-start.18) | collective-permute-done | bytes 163872 | tf_op jit(solution)/shard_map/ppermute | solution.py:120
  41.1 0.3 collective-permute-start.17
  41.4 1.1 %collective-permute-done.17.refs_13_ = bf16[4,16,1280]{2,1,0:T(8,128)(2,1)S(1)} collective-permute-done((bf16[4,16,1280]{2,1,0:T(8,128)(2,1)S(1)}, bf16[4,16,1280]{2,1,0:T(8,128)(2,1)S(1)}, u32[]{:S(2)}, u32[]{:S(2)}) %collective-permute-start.17) | collective-permute-done | bytes 163872 | tf_op jit(solution)/shard_map/ppermute | solution.py:120
  42.5 0.0 collective-permute-done.6.refs_4_
  42.5 0.0 collective-permute-done.9.refs_7_
  42.5 0.0 collective-permute-done.8.refs_6_
  42.5 0.0 collective-permute-done.7.refs_5_
  42.5 20.6 %contract.1 = f32[32,128]{1,0:T(8,128)S(1)} custom-call(bf16[4,16,2944]{2,1,0:T(8,128)(2,1)S(1)} %constant_dynamic-update-slice_fusion.refs_0_, bf16[4,16,2944]{2,1,0:T(8,128)(2,1)S(1)} %collective-permute-done.3.refs_1_, bf16[4,16,2944]{2,1,0:T(8,128)(2,1)S(1)} %collective-permute-done.4.refs_2_, bf16[4,16,2944]{2,1,0:T(8,128)(2,1)S(1)} %collective-permute-done.5.refs_3_, ...), custom_call_target="tpu_custom_call" | custom-call | flops 13153337344 | bytes 44040192 | tf_op jit(solution)/shard_map/contract/pallas_call | solution.py:338
  63.1 11.4 %all_to_all.9 = f32[32,1,128]{2,1,0:T(1,128)S(1)} all-to-all(f32[32,1,128]{2,1,0:T(1,128)S(1)} %bitcast.9), channel_id=1, replica_groups=mesh['dp'=2,'expert'=4,'mp'=4] {'dp','expert','mp'}, dimensions={0} | all-to-all | bytes 32768 | tf_op jit(solution)/shard_map/all_to_all | solution.py:184
  74.5 0.1 reduce_sum.9
  74.5 0.6 reshape.13
  (6 shorter events, 0.1 us)
Async XLA Ops:
  1.6 11.3 %collective-permute-start.12 = (bf16[1,16,1280]{2,1,0:T(8,128)(2,1)}, bf16[1,16,1280]{2,1,0:T(8,128)(2,1)S(1)}, u32[]{:S(2)}, u32[]{:S(2)}) collective-permute-start(bf16[1,16,1280]{2,1,0:T(8,128)(2,1)} %get-tuple-element.8), channel_id=1, source_target_pairs={{0,18},{1,19},{2,16},{3,17},{4,22},{5,23},{6,20},{7,21},{8,26},{9,... | collective-permute-start | bytes 122888 | tf_op jit(solution)/shard_map/ppermute | solution.py:120
  5.5 7.4 %collective-permute-start.11 = (bf16[1,16,1280]{2,1,0:T(8,128)(2,1)}, bf16[1,16,1280]{2,1,0:T(8,128)(2,1)S(1)}, u32[]{:S(2)}, u32[]{:S(2)}) collective-permute-start(bf16[1,16,1280]{2,1,0:T(8,128)(2,1)} %get-tuple-element.8), channel_id=1, source_target_pairs={{0,16},{1,17},{2,18},{3,19},{4,20},{5,21},{6,22},{7,23},{8,24},{9,... | collective-permute-start | bytes 122888 | tf_op jit(solution)/shard_map/ppermute | solution.py:120
  6.0 5.9 %collective-permute-start.10 = (bf16[1,16,1280]{2,1,0:T(8,128)(2,1)}, bf16[1,16,1280]{2,1,0:T(8,128)(2,1)S(1)}, u32[]{:S(2)}, u32[]{:S(2)}) collective-permute-start(bf16[1,16,1280]{2,1,0:T(8,128)(2,1)} %get-tuple-element.8), channel_id=1, source_target_pairs={{0,2},{1,3},{2,0},{3,1},{4,6},{5,7},{6,4},{7,5},{8,10},{9,11},{10,... | collective-permute-start | bytes 122888 | tf_op jit(solution)/shard_map/ppermute | solution.py:120
  6.1 12.5 %collective-permute-start.2 = (bf16[1,16,2944]{2,1,0:T(8,128)(2,1)}, bf16[1,16,2944]{2,1,0:T(8,128)(2,1)S(1)}, u32[]{:S(2)}, u32[]{:S(2)}) collective-permute-start(bf16[1,16,2944]{2,1,0:T(8,128)(2,1)} %get-tuple-element.7), channel_id=1, source_target_pairs={{0,12},{1,13},{2,14},{3,15},{4,0},{5,1},{6,2},{7,3},{8,4},{9,5},{1... | collective-permute-start | bytes 282632 | tf_op jit(solution)/shard_map/ppermute | solution.py:120
  10.2 8.4 %collective-permute-start.1 = (bf16[1,16,2944]{2,1,0:T(8,128)(2,1)}, bf16[1,16,2944]{2,1,0:T(8,128)(2,1)S(1)}, u32[]{:S(2)}, u32[]{:S(2)}) collective-permute-start(bf16[1,16,2944]{2,1,0:T(8,128)(2,1)} %get-tuple-element.7), channel_id=1, source_target_pairs={{0,8},{1,9},{2,10},{3,11},{4,12},{5,13},{6,14},{7,15},{8,0},{9,1},... | collective-permute-start | bytes 282632 | tf_op jit(solution)/shard_map/ppermute | solution.py:120
  11.9 6.6 %collective-permute-start = (bf16[1,16,2944]{2,1,0:T(8,128)(2,1)}, bf16[1,16,2944]{2,1,0:T(8,128)(2,1)S(1)}, u32[]{:S(2)}, u32[]{:S(2)}) collective-permute-start(bf16[1,16,2944]{2,1,0:T(8,128)(2,1)} %get-tuple-element.7), channel_id=1, source_target_pairs={{0,4},{1,5},{2,6},{3,7},{4,8},{5,9},{6,10},{7,11},{8,12},{9,13},{1... | collective-permute-start | bytes 282632 | tf_op jit(solution)/shard_map/ppermute | solution.py:120
  12.9 10.7 %collective-permute-start.16 = (bf16[4,16,1280]{2,1,0:T(8,128)(2,1)S(1)}, bf16[4,16,1280]{2,1,0:T(8,128)(2,1)S(1)}, u32[]{:S(2)}, u32[]{:S(2)}) collective-permute-start(bf16[4,16,1280]{2,1,0:T(8,128)(2,1)S(1)} %constant_dynamic-update-slice_fusion.4.refs_8_), channel_id=1, source_target_pairs={{0,1},{1,0},{2,3},{3,2},{4,5},{5,4},{6,7},{7,6},{8,9},{9,8},{10,11... | collective-permute-start | bytes 491528 | tf_op jit(solution)/shard_map/ppermute | solution.py:120
  18.6 19.3 %collective-permute-start.5 = (bf16[4,16,2944]{2,1,0:T(8,128)(2,1)S(1)}, bf16[4,16,2944]{2,1,0:T(8,128)(2,1)S(1)}, u32[]{:S(2)}, u32[]{:S(2)}) collective-permute-start(bf16[4,16,2944]{2,1,0:T(8,128)(2,1)S(1)} %constant_dynamic-update-slice_fusion.refs_0_), channel_id=1, source_target_pairs={{0,18},{1,19},{2,16},{3,17},{4,22},{5,23},{6,20},{7,21},{8,26},{9,... | collective-permute-start | bytes 1130504 | tf_op jit(solution)/shard_map/ppermute | solution.py:120
  21.1 16.9 %collective-permute-start.4 = (bf16[4,16,2944]{2,1,0:T(8,128)(2,1)S(1)}, bf16[4,16,2944]{2,1,0:T(8,128)(2,1)S(1)}, u32[]{:S(2)}, u32[]{:S(2)}) collective-permute-start(bf16[4,16,2944]{2,1,0:T(8,128)(2,1)S(1)} %constant_dynamic-update-slice_fusion.refs_0_), channel_id=1, source_target_pairs={{0,16},{1,17},{2,18},{3,19},{4,20},{5,21},{6,22},{7,23},{8,24},{9,... | collective-permute-start | bytes 1130504 | tf_op jit(solution)/shard_map/ppermute | solution.py:120
  21.6 16.8 %collective-permute-start.3 = (bf16[4,16,2944]{2,1,0:T(8,128)(2,1)S(1)}, bf16[4,16,2944]{2,1,0:T(8,128)(2,1)S(1)}, u32[]{:S(2)}, u32[]{:S(2)}) collective-permute-start(bf16[4,16,2944]{2,1,0:T(8,128)(2,1)S(1)} %constant_dynamic-update-slice_fusion.refs_0_), channel_id=1, source_target_pairs={{0,2},{1,3},{2,0},{3,1},{4,6},{5,7},{6,4},{7,5},{8,10},{9,11},{10,... | collective-permute-start | bytes 1130504 | tf_op jit(solution)/shard_map/ppermute | solution.py:120
  22.1 6.1 %collective-permute-start.15 = (bf16[4,16,1280]{2,1,0:T(8,128)(2,1)S(1)}, bf16[4,16,1280]{2,1,0:T(8,128)(2,1)S(1)}, u32[]{:S(2)}, u32[]{:S(2)}) collective-permute-start(bf16[4,16,1280]{2,1,0:T(8,128)(2,1)S(1)} %constant_dynamic-update-slice_fusion.4.refs_8_), channel_id=1, source_target_pairs={{0,12},{1,13},{2,14},{3,15},{4,0},{5,1},{6,2},{7,3},{8,4},{9,5},{1... | collective-permute-start | bytes 491528 | tf_op jit(solution)/shard_map/ppermute | solution.py:120
  23.6 13.7 %collective-permute-start.14 = (bf16[4,16,1280]{2,1,0:T(8,128)(2,1)S(1)}, bf16[4,16,1280]{2,1,0:T(8,128)(2,1)S(1)}, u32[]{:S(2)}, u32[]{:S(2)}) collective-permute-start(bf16[4,16,1280]{2,1,0:T(8,128)(2,1)S(1)} %constant_dynamic-update-slice_fusion.4.refs_8_), channel_id=1, source_target_pairs={{0,8},{1,9},{2,10},{3,11},{4,12},{5,13},{6,14},{7,15},{8,0},{9,1},... | collective-permute-start | bytes 491528 | tf_op jit(solution)/shard_map/ppermute | solution.py:120
  28.2 9.2 %collective-permute-start.13 = (bf16[4,16,1280]{2,1,0:T(8,128)(2,1)S(1)}, bf16[4,16,1280]{2,1,0:T(8,128)(2,1)S(1)}, u32[]{:S(2)}, u32[]{:S(2)}) collective-permute-start(bf16[4,16,1280]{2,1,0:T(8,128)(2,1)S(1)} %constant_dynamic-update-slice_fusion.4.refs_8_), channel_id=1, source_target_pairs={{0,4},{1,5},{2,6},{3,7},{4,8},{5,9},{6,10},{7,11},{8,12},{9,13},{1... | collective-permute-start | bytes 491528 | tf_op jit(solution)/shard_map/ppermute | solution.py:120
  37.3 1.4 %collective-permute-start.19 = (bf16[4,16,1280]{2,1,0:T(8,128)(2,1)S(1)}, bf16[4,16,1280]{2,1,0:T(8,128)(2,1)S(1)}, u32[]{:S(2)}, u32[]{:S(2)}) collective-permute-start(bf16[4,16,1280]{2,1,0:T(8,128)(2,1)S(1)} %collective-permute-done.15.refs_11_), channel_id=1, source_target_pairs={{0,1},{1,0},{2,3},{3,2},{4,5},{5,4},{6,7},{7,6},{8,9},{9,8},{10,11... | collective-permute-start | bytes 491528 | tf_op jit(solution)/shard_map/ppermute | solution.py:120
  37.3 5.2 %collective-permute-start.6 = (bf16[4,16,2944]{2,1,0:T(8,128)(2,1)S(1)}, bf16[4,16,2944]{2,1,0:T(8,128)(2,1)S(1)}, u32[]{:S(2)}, u32[]{:S(2)}) collective-permute-start(bf16[4,16,2944]{2,1,0:T(8,128)(2,1)S(1)} %constant_dynamic-update-slice_fusion.refs_0_), channel_id=1, source_target_pairs={{0,1},{1,0},{2,3},{3,2},{4,5},{5,4},{6,7},{7,6},{8,9},{9,8},{10,11... | collective-permute-start | bytes 1130504 | tf_op jit(solution)/shard_map/ppermute | solution.py:120
  37.9 4.7 %collective-permute-start.9 = (bf16[4,16,2944]{2,1,0:T(8,128)(2,1)S(1)}, bf16[4,16,2944]{2,1,0:T(8,128)(2,1)S(1)}, u32[]{:S(2)}, u32[]{:S(2)}) collective-permute-start(bf16[4,16,2944]{2,1,0:T(8,128)(2,1)S(1)} %collective-permute-done.5.refs_3_), channel_id=1, source_target_pairs={{0,1},{1,0},{2,3},{3,2},{4,5},{5,4},{6,7},{7,6},{8,9},{9,8},{10,11... | collective-permute-start | bytes 1130504 | tf_op jit(solution)/shard_map/ppermute | solution.py:120
  37.9 4.6 %collective-permute-start.8 = (bf16[4,16,2944]{2,1,0:T(8,128)(2,1)S(1)}, bf16[4,16,2944]{2,1,0:T(8,128)(2,1)S(1)}, u32[]{:S(2)}, u32[]{:S(2)}) collective-permute-start(bf16[4,16,2944]{2,1,0:T(8,128)(2,1)S(1)} %collective-permute-done.4.refs_2_), channel_id=1, source_target_pairs={{0,1},{1,0},{2,3},{3,2},{4,5},{5,4},{6,7},{7,6},{8,9},{9,8},{10,11... | collective-permute-start | bytes 1130504 | tf_op jit(solution)/shard_map/ppermute | solution.py:120
  38.4 4.2 %collective-permute-start.7 = (bf16[4,16,2944]{2,1,0:T(8,128)(2,1)S(1)}, bf16[4,16,2944]{2,1,0:T(8,128)(2,1)S(1)}, u32[]{:S(2)}, u32[]{:S(2)}) collective-permute-start(bf16[4,16,2944]{2,1,0:T(8,128)(2,1)S(1)} %collective-permute-done.3.refs_1_), channel_id=1, source_target_pairs={{0,1},{1,0},{2,3},{3,2},{4,5},{5,4},{6,7},{7,6},{8,9},{9,8},{10,11... | collective-permute-start | bytes 1130504 | tf_op jit(solution)/shard_map/ppermute | solution.py:120
  38.7 2.4 %collective-permute-start.18 = (bf16[4,16,1280]{2,1,0:T(8,128)(2,1)S(1)}, bf16[4,16,1280]{2,1,0:T(8,128)(2,1)S(1)}, u32[]{:S(2)}, u32[]{:S(2)}) collective-permute-start(bf16[4,16,1280]{2,1,0:T(8,128)(2,1)S(1)} %collective-permute-done.14.refs_10_), channel_id=1, source_target_pairs={{0,1},{1,0},{2,3},{3,2},{4,5},{5,4},{6,7},{7,6},{8,9},{9,8},{10,11... | collective-permute-start | bytes 491528 | tf_op jit(solution)/shard_map/ppermute | solution.py:120
  41.1 1.4 %collective-permute-start.17 = (bf16[4,16,1280]{2,1,0:T(8,128)(2,1)S(1)}, bf16[4,16,1280]{2,1,0:T(8,128)(2,1)S(1)}, u32[]{:S(2)}, u32[]{:S(2)}) collective-permute-start(bf16[4,16,1280]{2,1,0:T(8,128)(2,1)S(1)} %collective-permute-done.13.refs_9_), channel_id=1, source_target_pairs={{0,1},{1,0},{2,3},{3,2},{4,5},{5,4},{6,7},{7,6},{8,9},{9,8},{10,11... | collective-permute-start | bytes 491528 | tf_op jit(solution)/shard_map/ppermute | solution.py:120

commit v3 on v2

--- a/solution.py
+++ b/solution.py
@@ -9,7 +9,7 @@
 LANES = 128
 FF_TILE = 256
 COLUMNS = 256
-CUT = 22
+CUT = 24
 SLOTS = 3
 KINDS = 4
 VMEM_ROWS = 16 * 1024 * 1024
@@ -176,9 +176,19 @@
         tok_dev, width = tokens.shape
         probe_count = probes.shape[0]
         a, b = pack(tokens, probes, cotangent, expert_ids, combine, width * CUT // 32)
-        a = join(over_z(a))
+        a = over_z(a)
         b = join(over_plane(b))
-        a = over_core(over_plane(a))
+        middle = LANES + (a[0].shape[2] - LANES) // 2
+        low = join([p[:, :, :middle] for p in a])
+        high = join([p[:, :, middle:] for p in a])
+        low_x = send(low, 1, 0, 0, 0)
+        high_y = send(high, 0, 0, 1, 0)
+        high_x = send(high, 1, 0, 0, 0)
+        low_y = send(low, 0, 0, 1, 0)
+        low_far = send(low_x, 0, 0, 1, 0)
+        high_far = send(high_y, 1, 0, 0, 0)
+        a = [low, high, low_y, high_y, low_x, high_x, low_far, high_far]
+        a = over_core(a)
         b = over_core(over_z(b))
         partial = contract(a, b, w_gate[0], w_up[0], w_down[0], tok_dev, expert_ids.shape[1])
         swapped = lax.all_to_all(partial, AXES, split_axis=0, concat_axis=0, tiled=True)
@@ -230,10 +240,11 @@
             expert = lax.axis_index("expert").astype(jnp.float32)
             count = len(plane_shifts)
             for core in range(lay.core):
-                mine = pieces[core * count : (core + 1) * count]
-                late = pieces[2 * count + core * group : 2 * count + (core + 1) * group]
+                mine = pieces[core * 2 * count : (core + 1) * 2 * count]
+                late = pieces[4 * count + core * group : 4 * count + (core + 1) * group]
                 for j in range(count):
-                    early = [(mine[j], dz) for dz in range(group)]
+                    early = [(mine[2 * j], dz) for dz in range(group)]
+                    next_half = [(mine[2 * j + 1], dz) for dz in range(group)]
                     base = (core * count + j) * size
                     tags = split(early, 0, LANES)[0]
                     weight = jnp.zeros((size, 1), jnp.float32)
@@ -249,9 +260,12 @@
                         for kind in range(KINDS):
                             lhs[pl.ds(kind * rows + base, size), pl.ds(to, COLUMNS)] = parts[kind].astype(jnp.bfloat16)
 
-                    cut = mine[0].shape[2] - LANES
-                    for k in range(cut // COLUMNS):
+                    part = mine[1].shape[2]
+                    cut = 2 * part
+                    for k in range(part // COLUMNS):
                         take(early, LANES + k * COLUMNS, k * COLUMNS)
+                    for k in range(part // COLUMNS):
+                        take(next_half, k * COLUMNS, part + k * COLUMNS)
                     for k in range((width - cut) // COLUMNS):
                         take([(late[dz], j) for dz in range(group)], k * COLUMNS, cut + k * COLUMNS)
 
@@ -366,7 +380,8 @@
     rows = (probes.shape[0] + 2) * tokens.shape[0]
     tok_dev = tokens.shape[0] // mesh.size
     return (
-        mesh.shape["mp"] % 2 == 0
+        mesh.shape["mp"] == 4
+        and mesh.shape["dp"] == 2
         and w_gate.shape[0] == mesh.shape["expert"]
         and probes.shape[0] + 2 == KINDS
         and tok_dev == 4

time: 75.4 us -> 81.1 us (1.076)
  waiting for transfers between devices: 16.4 us -> 23.9 us
  blocking collectives: 11.4 us -> 8.88 us
    ppermute x20 -> x27, waiting for transfers between devices: 16.4 us -> 23.9 us  [send(): return lax.ppermute(block, AXES, lay.pairs(dx, dz, dy, dc))]
    all_to_all x1, blocking collectives: 11.4 us -> 8.88 us  [staged(): lax.all_to_all(partial, AXES, split_axis=0, concat_axis=0, tiled=True)]
    slice x0 -> x8, local copies, waits for them, and re-layouts: none -> 1.64 us  [the longest x4 0.83 us: staged(): low = join([p[:, :, :middle] for p in a])]
    unnamed x6 -> x3, local copies, waits for them, and re-layouts: 1.78 us -> 0.77 us
    ppermute x20 -> x27, starting transfers between devices: 22.7 us -> 22.5 us  [send(): return lax.ppermute(block, AXES, lay.pairs(dx, dz, dy, dc))]
  transfers between devices with their start and end apart: 20 -> 27, of which waited for: 6 -> 10; matrix products, arithmetic and copies ran while one was open for 2% -> 3% of each run, Pallas kernels for 0% -> 0%
where the time goes in v3:
time: 81.1 us; the launch traced here: 80.7 us
  waiting for transfers between devices  23.9 us (29%)
  starting transfers between devices  22.5 us (28%)
  Pallas kernels  22.1 us (27%)
  blocking collectives  8.88 us (11%)
  local copies, waits for them, and re-layouts  3.06 us (4%)
    ppermute x27, waiting for transfers between devices, send(): return lax.ppermute(block, AXES, lay.pairs(dx, dz, dy, dc))  23.9 us
    ppermute x27, starting transfers between devices, send(): return lax.ppermute(block, AXES, lay.pairs(dx, dz, dy, dc))  22.5 us
    pallas_call x1, Pallas kernels, contract(): pl.pallas_call(body, out_shape=jax.ShapeDtypeStruct((2 * half, LANES), f3...  20.5 us
    all_to_all x1, blocking collectives, staged(): lax.all_to_all(partial, AXES, split_axis=0, concat_axis=0, tiled=True)  8.88 us
  transfers between devices with their start and end apart: 27, of which 10 were waited for; matrix products, arithmetic and copies ran while one was open for 3% of the time, Pallas kernels for 0%

profile of v3, /device:TPU:0, one launch (start us, length us, event | category | flops | bytes accessed | tf_op | source)
XLA Modules:
  0.0 80.7 jit_solution(12081190880987292346)
XLA Ops:
  0.0 1.6 %pack.1 = (bf16[1,16,3200]{2,1,0:T(8,128)(2,1)}, bf16[1,16,1024]{2,1,0:T(8,128)(2,1)}) custom-call(bf16[4,4096]{1,0:T(4,128)(2,1)} %tok_ref.1, bf16[2,4,4096]{2,1,0:T(4,128)(2,1)} %probe_ref.1, bf16[4,4096]{1,0:T(4,128)(2,1)} %cot_ref.1, s32[2,4]{1,0:T(2,128)} %bitcast.10, f32[2,4]{1,0:T(2,128)} %bitcast.11), custom_call_target="tpu_custom_call" | custom-call | tf_op jit(solution)/shard_map/pack/pallas_call | solution.py:163
  1.6 3.9 %collective-permute-start.19 = (bf16[1,16,1024]{2,1,0:T(8,128)(2,1)}, bf16[1,16,1024]{2,1,0:T(8,128)(2,1)S(1)}, u32[]{:S(2)}, u32[]{:S(2)}) collective-permute-start(bf16[1,16,1024]{2,1,0:T(8,128)(2,1)} %get-tuple-element.8), channel_id=1, source_target_pairs={{0,18},{1,19},{2,16},{3,17},{4,22},{5,23},{6,20},{7,21},{8,26},{9,... | collective-permute-start | bytes 98312 | tf_op jit(solution)/shard_map/ppermute | solution.py:120
  5.5 0.5 collective-permute-start.18
  6.0 0.0 collective-permute-start.17
  6.1 4.1 %collective-permute-start.2 = (bf16[1,16,3200]{2,1,0:T(8,128)(2,1)}, bf16[1,16,3200]{2,1,0:T(8,128)(2,1)S(1)}, u32[]{:S(2)}, u32[]{:S(2)}) collective-permute-start(bf16[1,16,3200]{2,1,0:T(8,128)(2,1)} %get-tuple-element.7), channel_id=1, source_target_pairs={{0,12},{1,13},{2,14},{3,15},{4,0},{5,1},{6,2},{7,3},{8,4},{9,5},{1... | collective-permute-start | bytes 307208 | tf_op jit(solution)/shard_map/ppermute | solution.py:120
  10.1 0.8 constant_dynamic-update-slice_fusion.3
  10.9 0.8 slice.39
  11.7 0.8 %slice.35 = bf16[1,16,1664]{2,1,0:T(8,128)(2,1)S(1)} slice(bf16[1,16,3200]{2,1,0:T(8,128)(2,1)} %get-tuple-element.7), slice={[0:1], [0:16], [0:1664]} | slice | bytes 106496 | tf_op jit(solution)/shard_map/slice | solution.py:182
  12.5 1.0 %collective-permute-start = (bf16[1,16,3200]{2,1,0:T(8,128)(2,1)}, bf16[1,16,3200]{2,1,0:T(8,128)(2,1)S(1)}, u32[]{:S(2)}, u32[]{:S(2)}) collective-permute-start(bf16[1,16,3200]{2,1,0:T(8,128)(2,1)} %get-tuple-element.7), channel_id=1, source_target_pairs={{0,4},{1,5},{2,6},{3,7},{4,8},{5,9},{6,10},{7,11},{8,12},{9,13},{1... | collective-permute-start | bytes 307208 | tf_op jit(solution)/shard_map/ppermute | solution.py:120
  13.5 0.0 collective-permute-done.18
  13.5 0.0 collective-permute-done.19
  13.6 0.1 collective-permute-start.23
  13.6 2.9 %collective-permute-start.22 = (bf16[4,16,1024]{2,1,0:T(8,128)(2,1)S(1)}, bf16[4,16,1024]{2,1,0:T(8,128)(2,1)S(1)}, u32[]{:S(2)}, u32[]{:S(2)}) collective-permute-start(bf16[4,16,1024]{2,1,0:T(8,128)(2,1)S(1)} %constant_dynamic-update-slice_fusion.refs_16_), channel_id=1, source_target_pairs={{0,12},{1,13},{2,14},{3,15},{4,0},{5,1},{6,2},{7,3},{8,4},{9,5},{1... | collective-permute-start | bytes 393224 | tf_op jit(solution)/shard_map/ppermute | solution.py:120
  16.5 0.0 collective-permute-done.2
  16.5 1.1 %collective-permute-start.21 = (bf16[4,16,1024]{2,1,0:T(8,128)(2,1)S(1)}, bf16[4,16,1024]{2,1,0:T(8,128)(2,1)S(1)}, u32[]{:S(2)}, u32[]{:S(2)}) collective-permute-start(bf16[4,16,1024]{2,1,0:T(8,128)(2,1)S(1)} %constant_dynamic-update-slice_fusion.refs_16_), channel_id=1, source_target_pairs={{0,8},{1,9},{2,10},{3,11},{4,12},{5,13},{6,14},{7,15},{8,0},{9,1},... | collective-permute-start | bytes 393224 | tf_op jit(solution)/shard_map/ppermute | solution.py:120
  17.6 0.3 collective-permute-done.1
  18.0 0.3 collective-permute-start.20
  18.3 2.0 %collective-permute-done = bf16[1,16,3200]{2,1,0:T(8,128)(2,1)S(1)} collective-permute-done((bf16[1,16,3200]{2,1,0:T(8,128)(2,1)}, bf16[1,16,3200]{2,1,0:T(8,128)(2,1)S(1)}, u32[]{:S(2)}, u32[]{:S(2)}) %collective-permute-start) | collective-permute-done | bytes 102432 | tf_op jit(solution)/shard_map/ppermute | solution.py:120
  20.3 1.6 %collective-permute-start.5 = (bf16[4,16,1664]{2,1,0:T(8,128)(2,1)S(1)}, bf16[4,16,1664]{2,1,0:T(8,128)(2,1)S(1)}, u32[]{:S(2)}, u32[]{:S(2)}) collective-permute-start(bf16[4,16,1664]{2,1,0:T(8,128)(2,1)S(1)} %pad_maximum_fusion.refs_0_), channel_id=1, source_target_pairs={{0,16},{1,17},{2,18},{3,19},{4,20},{5,21},{6,22},{7,23},{8,24},{9,... | collective-permute-start | bytes 638984 | tf_op jit(solution)/shard_map/ppermute | solution.py:120
  21.9 0.0 collective-permute-done.22.refs_19_
  21.9 0.1 collective-permute-start.26
  22.0 8.7 %collective-permute-done.21.refs_18_ = bf16[4,16,1024]{2,1,0:T(8,128)(2,1)S(1)} collective-permute-done((bf16[4,16,1024]{2,1,0:T(8,128)(2,1)S(1)}, bf16[4,16,1024]{2,1,0:T(8,128)(2,1)S(1)}, u32[]{:S(2)}, u32[]{:S(2)}) %collective-permute-start.21) | collective-permute-done | bytes 131104 | tf_op jit(solution)/shard_map/ppermute | solution.py:120
  30.7 0.6 collective-permute-start.10
  31.3 0.0 collective-permute-done.20.refs_17_
  31.3 1.5 %collective-permute-start.6 = (bf16[4,16,1536]{2,1,0:T(8,128)(2,1)S(1)}, bf16[4,16,1536]{2,1,0:T(8,128)(2,1)S(1)}, u32[]{:S(2)}, u32[]{:S(2)}) collective-permute-start(bf16[4,16,1536]{2,1,0:T(8,128)(2,1)S(1)} %pad_maximum_fusion.1.refs_1_), channel_id=1, source_target_pairs={{0,16},{1,17},{2,18},{3,19},{4,20},{5,21},{6,22},{7,23},{8,24},{9,... | collective-permute-start | bytes 589832 | tf_op jit(solution)/shard_map/ppermute | solution.py:120
  32.8 0.0 collective-permute-done.26.refs_23_
  32.8 1.5 %collective-permute-start.4 = (bf16[4,16,1536]{2,1,0:T(8,128)(2,1)S(1)}, bf16[4,16,1536]{2,1,0:T(8,128)(2,1)S(1)}, u32[]{:S(2)}, u32[]{:S(2)}) collective-permute-start(bf16[4,16,1536]{2,1,0:T(8,128)(2,1)S(1)} %pad_maximum_fusion.1.refs_1_), channel_id=1, source_target_pairs={{0,2},{1,3},{2,0},{3,1},{4,6},{5,7},{6,4},{7,5},{8,10},{9,11},{10,... | collective-permute-start | bytes 589832 | tf_op jit(solution)/shard_map/ppermute | solution.py:120
  34.3 0.0 collective-permute-done.25.refs_22_
  34.3 0.0 collective-permute-start.24
  34.3 1.3 %collective-permute-done.24.refs_21_ = bf16[4,16,1024]{2,1,0:T(8,128)(2,1)S(1)} collective-permute-done((bf16[4,16,1024]{2,1,0:T(8,128)(2,1)S(1)}, bf16[4,16,1024]{2,1,0:T(8,128)(2,1)S(1)}, u32[]{:S(2)}, u32[]{:S(2)}) %collective-permute-start.24) | collective-permute-done | bytes 131104 | tf_op jit(solution)/shard_map/ppermute | solution.py:120
  35.7 0.1 collective-permute-start.9
  35.8 0.0 collective-permute-done.10.refs_9_
  35.8 0.5 collective-permute-start.3
  36.3 0.0 collective-permute-done.5.refs_4_
  36.3 1.5 %collective-permute-start.7 = (bf16[4,16,1664]{2,1,0:T(8,128)(2,1)S(1)}, bf16[4,16,1664]{2,1,0:T(8,128)(2,1)S(1)}, u32[]{:S(2)}, u32[]{:S(2)}) collective-permute-start(bf16[4,16,1664]{2,1,0:T(8,128)(2,1)S(1)} %collective-permute-done.5.refs_4_), channel_id=1, source_target_pairs={{0,2},{1,3},{2,0},{3,1},{4,6},{5,7},{6,4},{7,5},{8,10},{9,11},{10,... | collective-permute-start | bytes 638984 | tf_op jit(solution)/shard_map/ppermute | solution.py:120
  37.9 0.3 collective-permute-done.6.refs_5_
  38.2 1.8 %collective-permute-done.4.refs_3_ = bf16[4,16,1536]{2,1,0:T(8,128)(2,1)S(1)} collective-permute-done((bf16[4,16,1536]{2,1,0:T(8,128)(2,1)S(1)}, bf16[4,16,1536]{2,1,0:T(8,128)(2,1)S(1)}, u32[]{:S(2)}, u32[]{:S(2)}) %collective-permute-start.4) | collective-permute-done | bytes 196640 | tf_op jit(solution)/shard_map/ppermute | solution.py:120
  40.1 0.5 collective-permute-start.8
  40.6 4.0 %collective-permute-done.3.refs_2_ = bf16[4,16,1664]{2,1,0:T(8,128)(2,1)S(1)} collective-permute-done((bf16[4,16,1664]{2,1,0:T(8,128)(2,1)S(1)}, bf16[4,16,1664]{2,1,0:T(8,128)(2,1)S(1)}, u32[]{:S(2)}, u32[]{:S(2)}) %collective-permute-start.3) | collective-permute-done | bytes 213024 | tf_op jit(solution)/shard_map/ppermute | solution.py:120
  44.6 3.9 %collective-permute-done.7.refs_6_ = bf16[4,16,1664]{2,1,0:T(8,128)(2,1)S(1)} collective-permute-done((bf16[4,16,1664]{2,1,0:T(8,128)(2,1)S(1)}, bf16[4,16,1664]{2,1,0:T(8,128)(2,1)S(1)}, u32[]{:S(2)}, u32[]{:S(2)}) %collective-permute-start.7) | collective-permute-done | bytes 213024 | tf_op jit(solution)/shard_map/ppermute | solution.py:120
  48.6 0.5 collective-permute-start.12
  49.1 0.1 collective-permute-start.16
  49.1 1.2 %collective-permute-done.12.refs_11_ = bf16[4,16,1536]{2,1,0:T(8,128)(2,1)S(1)} collective-permute-done((bf16[4,16,1536]{2,1,0:T(8,128)(2,1)S(1)}, bf16[4,16,1536]{2,1,0:T(8,128)(2,1)S(1)}, u32[]{:S(2)}, u32[]{:S(2)}) %collective-permute-start.12) | collective-permute-done | bytes 196640 | tf_op jit(solution)/shard_map/ppermute | solution.py:120
  50.3 0.3 collective-permute-done.16.refs_15_
  50.6 20.5 %contract.1 = f32[32,128]{1,0:T(8,128)S(1)} custom-call(bf16[4,16,1664]{2,1,0:T(8,128)(2,1)S(1)} %pad_maximum_fusion.refs_0_, bf16[4,16,1536]{2,1,0:T(8,128)(2,1)S(1)} %pad_maximum_fusion.1.refs_1_, bf16[4,16,1664]{2,1,0:T(8,128)(2,1)S(1)} %collective-permute-done.3.refs_2_, bf16[4,16,1536]{2,1,0:T(8,128)(2,1)S(1)} %collective-permute-done.4.refs_3_, ...), custom_call_target="tpu_custom_call" | custom-call | flops 13153337344 | bytes 44040192 | tf_op jit(solution)/shard_map/contract/pallas_call | solution.py:352
  71.1 8.9 %all_to_all.9 = f32[32,1,128]{2,1,0:T(1,128)S(1)} all-to-all(f32[32,1,128]{2,1,0:T(1,128)S(1)} %bitcast.9), channel_id=1, replica_groups=mesh['dp'=2,'expert'=4,'mp'=4] {'dp','expert','mp'}, dimensions={0} | all-to-all | bytes 32768 | tf_op jit(solution)/shard_map/all_to_all | solution.py:194
  80.0 0.1 reduce_sum.9
  80.1 0.6 reshape.13
  (25 shorter events, 0.1 us)
Async XLA Ops:
  1.6 12.0 %collective-permute-start.19 = (bf16[1,16,1024]{2,1,0:T(8,128)(2,1)}, bf16[1,16,1024]{2,1,0:T(8,128)(2,1)S(1)}, u32[]{:S(2)}, u32[]{:S(2)}) collective-permute-start(bf16[1,16,1024]{2,1,0:T(8,128)(2,1)} %get-tuple-element.8), channel_id=1, source_target_pairs={{0,18},{1,19},{2,16},{3,17},{4,22},{5,23},{6,20},{7,21},{8,26},{9,... | collective-permute-start | bytes 98312 | tf_op jit(solution)/shard_map/ppermute | solution.py:120
  5.5 8.0 %collective-permute-start.18 = (bf16[1,16,1024]{2,1,0:T(8,128)(2,1)}, bf16[1,16,1024]{2,1,0:T(8,128)(2,1)S(1)}, u32[]{:S(2)}, u32[]{:S(2)}) collective-permute-start(bf16[1,16,1024]{2,1,0:T(8,128)(2,1)} %get-tuple-element.8), channel_id=1, source_target_pairs={{0,16},{1,17},{2,18},{3,19},{4,20},{5,21},{6,22},{7,23},{8,24},{9,... | collective-permute-start | bytes 98312 | tf_op jit(solution)/shard_map/ppermute | solution.py:120
  6.0 6.5 %collective-permute-start.17 = (bf16[1,16,1024]{2,1,0:T(8,128)(2,1)}, bf16[1,16,1024]{2,1,0:T(8,128)(2,1)S(1)}, u32[]{:S(2)}, u32[]{:S(2)}) collective-permute-start(bf16[1,16,1024]{2,1,0:T(8,128)(2,1)} %get-tuple-element.8), channel_id=1, source_target_pairs={{0,2},{1,3},{2,0},{3,1},{4,6},{5,7},{6,4},{7,5},{8,10},{9,11},{10,... | collective-permute-start | bytes 98312 | tf_op jit(solution)/shard_map/ppermute | solution.py:120
  6.1 10.5 %collective-permute-start.2 = (bf16[1,16,3200]{2,1,0:T(8,128)(2,1)}, bf16[1,16,3200]{2,1,0:T(8,128)(2,1)S(1)}, u32[]{:S(2)}, u32[]{:S(2)}) collective-permute-start(bf16[1,16,3200]{2,1,0:T(8,128)(2,1)} %get-tuple-element.7), channel_id=1, source_target_pairs={{0,12},{1,13},{2,14},{3,15},{4,0},{5,1},{6,2},{7,3},{8,4},{9,5},{1... | collective-permute-start | bytes 307208 | tf_op jit(solution)/shard_map/ppermute | solution.py:120
  10.1 7.8 %collective-permute-start.1 = (bf16[1,16,3200]{2,1,0:T(8,128)(2,1)}, bf16[1,16,3200]{2,1,0:T(8,128)(2,1)S(1)}, u32[]{:S(2)}, u32[]{:S(2)}) collective-permute-start(bf16[1,16,3200]{2,1,0:T(8,128)(2,1)} %get-tuple-element.7), channel_id=1, source_target_pairs={{0,8},{1,9},{2,10},{3,11},{4,12},{5,13},{6,14},{7,15},{8,0},{9,1},... | collective-permute-start | bytes 307208 | tf_op jit(solution)/shard_map/ppermute | solution.py:120
  12.5 7.7 %collective-permute-start = (bf16[1,16,3200]{2,1,0:T(8,128)(2,1)}, bf16[1,16,3200]{2,1,0:T(8,128)(2,1)S(1)}, u32[]{:S(2)}, u32[]{:S(2)}) collective-permute-start(bf16[1,16,3200]{2,1,0:T(8,128)(2,1)} %get-tuple-element.7), channel_id=1, source_target_pairs={{0,4},{1,5},{2,6},{3,7},{4,8},{5,9},{6,10},{7,11},{8,12},{9,13},{1... | collective-permute-start | bytes 307208 | tf_op jit(solution)/shard_map/ppermute | solution.py:120
  13.6 17.2 %collective-permute-start.23 = (bf16[4,16,1024]{2,1,0:T(8,128)(2,1)S(1)}, bf16[4,16,1024]{2,1,0:T(8,128)(2,1)S(1)}, u32[]{:S(2)}, u32[]{:S(2)}) collective-permute-start(bf16[4,16,1024]{2,1,0:T(8,128)(2,1)S(1)} %constant_dynamic-update-slice_fusion.refs_16_), channel_id=1, source_target_pairs={{0,1},{1,0},{2,3},{3,2},{4,5},{5,4},{6,7},{7,6},{8,9},{9,8},{10,11... | collective-permute-start | bytes 393224 | tf_op jit(solution)/shard_map/ppermute | solution.py:120
  13.6 8.2 %collective-permute-start.22 = (bf16[4,16,1024]{2,1,0:T(8,128)(2,1)S(1)}, bf16[4,16,1024]{2,1,0:T(8,128)(2,1)S(1)}, u32[]{:S(2)}, u32[]{:S(2)}) collective-permute-start(bf16[4,16,1024]{2,1,0:T(8,128)(2,1)S(1)} %constant_dynamic-update-slice_fusion.refs_16_), channel_id=1, source_target_pairs={{0,12},{1,13},{2,14},{3,15},{4,0},{5,1},{6,2},{7,3},{8,4},{9,5},{1... | collective-permute-start | bytes 393224 | tf_op jit(solution)/shard_map/ppermute | solution.py:120
  16.5 14.2 %collective-permute-start.21 = (bf16[4,16,1024]{2,1,0:T(8,128)(2,1)S(1)}, bf16[4,16,1024]{2,1,0:T(8,128)(2,1)S(1)}, u32[]{:S(2)}, u32[]{:S(2)}) collective-permute-start(bf16[4,16,1024]{2,1,0:T(8,128)(2,1)S(1)} %constant_dynamic-update-slice_fusion.refs_16_), channel_id=1, source_target_pairs={{0,8},{1,9},{2,10},{3,11},{4,12},{5,13},{6,14},{7,15},{8,0},{9,1},... | collective-permute-start | bytes 393224 | tf_op jit(solution)/shard_map/ppermute | solution.py:120
  18.0 13.4 %collective-permute-start.20 = (bf16[4,16,1024]{2,1,0:T(8,128)(2,1)S(1)}, bf16[4,16,1024]{2,1,0:T(8,128)(2,1)S(1)}, u32[]{:S(2)}, u32[]{:S(2)}) collective-permute-start(bf16[4,16,1024]{2,1,0:T(8,128)(2,1)S(1)} %constant_dynamic-update-slice_fusion.refs_16_), channel_id=1, source_target_pairs={{0,4},{1,5},{2,6},{3,7},{4,8},{5,9},{6,10},{7,11},{8,12},{9,13},{1... | collective-permute-start | bytes 393224 | tf_op jit(solution)/shard_map/ppermute | solution.py:120
  20.3 16.0 %collective-permute-start.5 = (bf16[4,16,1664]{2,1,0:T(8,128)(2,1)S(1)}, bf16[4,16,1664]{2,1,0:T(8,128)(2,1)S(1)}, u32[]{:S(2)}, u32[]{:S(2)}) collective-permute-start(bf16[4,16,1664]{2,1,0:T(8,128)(2,1)S(1)} %pad_maximum_fusion.refs_0_), channel_id=1, source_target_pairs={{0,16},{1,17},{2,18},{3,19},{4,20},{5,21},{6,22},{7,23},{8,24},{9,... | collective-permute-start | bytes 638984 | tf_op jit(solution)/shard_map/ppermute | solution.py:120
  21.9 10.9 %collective-permute-start.26 = (bf16[4,16,1024]{2,1,0:T(8,128)(2,1)S(1)}, bf16[4,16,1024]{2,1,0:T(8,128)(2,1)S(1)}, u32[]{:S(2)}, u32[]{:S(2)}) collective-permute-start(bf16[4,16,1024]{2,1,0:T(8,128)(2,1)S(1)} %collective-permute-done.22.refs_19_), channel_id=1, source_target_pairs={{0,1},{1,0},{2,3},{3,2},{4,5},{5,4},{6,7},{7,6},{8,9},{9,8},{10,11... | collective-permute-start | bytes 393224 | tf_op jit(solution)/shard_map/ppermute | solution.py:120
  30.7 3.6 %collective-permute-start.25 = (bf16[4,16,1024]{2,1,0:T(8,128)(2,1)S(1)}, bf16[4,16,1024]{2,1,0:T(8,128)(2,1)S(1)}, u32[]{:S(2)}, u32[]{:S(2)}) collective-permute-start(bf16[4,16,1024]{2,1,0:T(8,128)(2,1)S(1)} %collective-permute-done.21.refs_18_), channel_id=1, source_target_pairs={{0,1},{1,0},{2,3},{3,2},{4,5},{5,4},{6,7},{7,6},{8,9},{9,8},{10,11... | collective-permute-start | bytes 393224 | tf_op jit(solution)/shard_map/ppermute | solution.py:120
  30.7 5.1 %collective-permute-start.10 = (bf16[4,16,1536]{2,1,0:T(8,128)(2,1)S(1)}, bf16[4,16,1536]{2,1,0:T(8,128)(2,1)S(1)}, u32[]{:S(2)}, u32[]{:S(2)}) collective-permute-start(bf16[4,16,1536]{2,1,0:T(8,128)(2,1)S(1)} %pad_maximum_fusion.1.refs_1_), channel_id=1, source_target_pairs={{0,1},{1,0},{2,3},{3,2},{4,5},{5,4},{6,7},{7,6},{8,9},{9,8},{10,11... | collective-permute-start | bytes 589832 | tf_op jit(solution)/shard_map/ppermute | solution.py:120
  31.3 6.9 %collective-permute-start.6 = (bf16[4,16,1536]{2,1,0:T(8,128)(2,1)S(1)}, bf16[4,16,1536]{2,1,0:T(8,128)(2,1)S(1)}, u32[]{:S(2)}, u32[]{:S(2)}) collective-permute-start(bf16[4,16,1536]{2,1,0:T(8,128)(2,1)S(1)} %pad_maximum_fusion.1.refs_1_), channel_id=1, source_target_pairs={{0,16},{1,17},{2,18},{3,19},{4,20},{5,21},{6,22},{7,23},{8,24},{9,... | collective-permute-start | bytes 589832 | tf_op jit(solution)/shard_map/ppermute | solution.py:120
  32.8 7.2 %collective-permute-start.4 = (bf16[4,16,1536]{2,1,0:T(8,128)(2,1)S(1)}, bf16[4,16,1536]{2,1,0:T(8,128)(2,1)S(1)}, u32[]{:S(2)}, u32[]{:S(2)}) collective-permute-start(bf16[4,16,1536]{2,1,0:T(8,128)(2,1)S(1)} %pad_maximum_fusion.1.refs_1_), channel_id=1, source_target_pairs={{0,2},{1,3},{2,0},{3,1},{4,6},{5,7},{6,4},{7,5},{8,10},{9,11},{10,... | collective-permute-start | bytes 589832 | tf_op jit(solution)/shard_map/ppermute | solution.py:120
  34.3 1.3 %collective-permute-start.24 = (bf16[4,16,1024]{2,1,0:T(8,128)(2,1)S(1)}, bf16[4,16,1024]{2,1,0:T(8,128)(2,1)S(1)}, u32[]{:S(2)}, u32[]{:S(2)}) collective-permute-start(bf16[4,16,1024]{2,1,0:T(8,128)(2,1)S(1)} %collective-permute-done.20.refs_17_), channel_id=1, source_target_pairs={{0,1},{1,0},{2,3},{3,2},{4,5},{5,4},{6,7},{7,6},{8,9},{9,8},{10,11... | collective-permute-start | bytes 393224 | tf_op jit(solution)/shard_map/ppermute | solution.py:120
  35.7 4.9 %collective-permute-start.9 = (bf16[4,16,1664]{2,1,0:T(8,128)(2,1)S(1)}, bf16[4,16,1664]{2,1,0:T(8,128)(2,1)S(1)}, u32[]{:S(2)}, u32[]{:S(2)}) collective-permute-start(bf16[4,16,1664]{2,1,0:T(8,128)(2,1)S(1)} %pad_maximum_fusion.refs_0_), channel_id=1, source_target_pairs={{0,1},{1,0},{2,3},{3,2},{4,5},{5,4},{6,7},{7,6},{8,9},{9,8},{10,11... | collective-permute-start | bytes 638984 | tf_op jit(solution)/shard_map/ppermute | solution.py:120
  35.8 8.8 %collective-permute-start.3 = (bf16[4,16,1664]{2,1,0:T(8,128)(2,1)S(1)}, bf16[4,16,1664]{2,1,0:T(8,128)(2,1)S(1)}, u32[]{:S(2)}, u32[]{:S(2)}) collective-permute-start(bf16[4,16,1664]{2,1,0:T(8,128)(2,1)S(1)} %pad_maximum_fusion.refs_0_), channel_id=1, source_target_pairs={{0,2},{1,3},{2,0},{3,1},{4,6},{5,7},{6,4},{7,5},{8,10},{9,11},{10,... | collective-permute-start | bytes 638984 | tf_op jit(solution)/shard_map/ppermute | solution.py:120
  36.3 12.2 %collective-permute-start.7 = (bf16[4,16,1664]{2,1,0:T(8,128)(2,1)S(1)}, bf16[4,16,1664]{2,1,0:T(8,128)(2,1)S(1)}, u32[]{:S(2)}, u32[]{:S(2)}) collective-permute-start(bf16[4,16,1664]{2,1,0:T(8,128)(2,1)S(1)} %collective-permute-done.5.refs_4_), channel_id=1, source_target_pairs={{0,2},{1,3},{2,0},{3,1},{4,6},{5,7},{6,4},{7,5},{8,10},{9,11},{10,... | collective-permute-start | bytes 638984 | tf_op jit(solution)/shard_map/ppermute | solution.py:120
  38.2 10.3 %collective-permute-start.14 = (bf16[4,16,1536]{2,1,0:T(8,128)(2,1)S(1)}, bf16[4,16,1536]{2,1,0:T(8,128)(2,1)S(1)}, u32[]{:S(2)}, u32[]{:S(2)}) collective-permute-start(bf16[4,16,1536]{2,1,0:T(8,128)(2,1)S(1)} %collective-permute-done.6.refs_5_), channel_id=1, source_target_pairs={{0,1},{1,0},{2,3},{3,2},{4,5},{5,4},{6,7},{7,6},{8,9},{9,8},{10,11... | collective-permute-start | bytes 589832 | tf_op jit(solution)/shard_map/ppermute | solution.py:120
  40.1 9.0 %collective-permute-start.8 = (bf16[4,16,1536]{2,1,0:T(8,128)(2,1)S(1)}, bf16[4,16,1536]{2,1,0:T(8,128)(2,1)S(1)}, u32[]{:S(2)}, u32[]{:S(2)}) collective-permute-start(bf16[4,16,1536]{2,1,0:T(8,128)(2,1)S(1)} %collective-permute-done.4.refs_3_), channel_id=1, source_target_pairs={{0,16},{1,17},{2,18},{3,19},{4,20},{5,21},{6,22},{7,23},{8,24},{9,... | collective-permute-start | bytes 589832 | tf_op jit(solution)/shard_map/ppermute | solution.py:120
  40.6 9.7 %collective-permute-start.13 = (bf16[4,16,1664]{2,1,0:T(8,128)(2,1)S(1)}, bf16[4,16,1664]{2,1,0:T(8,128)(2,1)S(1)}, u32[]{:S(2)}, u32[]{:S(2)}) collective-permute-start(bf16[4,16,1664]{2,1,0:T(8,128)(2,1)S(1)} %collective-permute-done.5.refs_4_), channel_id=1, source_target_pairs={{0,1},{1,0},{2,3},{3,2},{4,5},{5,4},{6,7},{7,6},{8,9},{9,8},{10,11... | collective-permute-start | bytes 638984 | tf_op jit(solution)/shard_map/ppermute | solution.py:120
  44.6 5.7 %collective-permute-start.11 = (bf16[4,16,1664]{2,1,0:T(8,128)(2,1)S(1)}, bf16[4,16,1664]{2,1,0:T(8,128)(2,1)S(1)}, u32[]{:S(2)}, u32[]{:S(2)}) collective-permute-start(bf16[4,16,1664]{2,1,0:T(8,128)(2,1)S(1)} %collective-permute-done.3.refs_2_), channel_id=1, source_target_pairs={{0,1},{1,0},{2,3},{3,2},{4,5},{5,4},{6,7},{7,6},{8,9},{9,8},{10,11... | collective-permute-start | bytes 638984 | tf_op jit(solution)/shard_map/ppermute | solution.py:120
  48.5 2.0 %collective-permute-start.15 = (bf16[4,16,1664]{2,1,0:T(8,128)(2,1)S(1)}, bf16[4,16,1664]{2,1,0:T(8,128)(2,1)S(1)}, u32[]{:S(2)}, u32[]{:S(2)}) collective-permute-start(bf16[4,16,1664]{2,1,0:T(8,128)(2,1)S(1)} %collective-permute-done.7.refs_6_), channel_id=1, source_target_pairs={{0,1},{1,0},{2,3},{3,2},{4,5},{5,4},{6,7},{7,6},{8,9},{9,8},{10,11... | collective-permute-start | bytes 638984 | tf_op jit(solution)/shard_map/ppermute | solution.py:120
  48.6 1.7 %collective-permute-start.12 = (bf16[4,16,1536]{2,1,0:T(8,128)(2,1)S(1)}, bf16[4,16,1536]{2,1,0:T(8,128)(2,1)S(1)}, u32[]{:S(2)}, u32[]{:S(2)}) collective-permute-start(bf16[4,16,1536]{2,1,0:T(8,128)(2,1)S(1)} %collective-permute-done.4.refs_3_), channel_id=1, source_target_pairs={{0,1},{1,0},{2,3},{3,2},{4,5},{5,4},{6,7},{7,6},{8,9},{9,8},{10,11... | collective-permute-start | bytes 589832 | tf_op jit(solution)/shard_map/ppermute | solution.py:120
  49.1 1.5 %collective-permute-start.16 = (bf16[4,16,1536]{2,1,0:T(8,128)(2,1)S(1)}, bf16[4,16,1536]{2,1,0:T(8,128)(2,1)S(1)}, u32[]{:S(2)}, u32[]{:S(2)}) collective-permute-start(bf16[4,16,1536]{2,1,0:T(8,128)(2,1)S(1)} %collective-permute-done.8.refs_7_), channel_id=1, source_target_pairs={{0,1},{1,0},{2,3},{3,2},{4,5},{5,4},{6,7},{7,6},{8,9},{9,8},{10,11... | collective-permute-start | bytes 589832 | tf_op jit(solution)/shard_map/ppermute | solution.py:120
